TPU v7x, 512 devices: a whole 4x4x16 slice. The times are simulated.
512 devices in a mesh: row: 32 (over x, y, core), col: 16 (over z).
Axes of the slice: x: 4, y: 4, z: 16, core: 2. Of those that a mesh axis runs over, the one named last changes fastest.
Arguments:
- right_side: float32 [5, 32, 16, 32, 128], P(None, 'row', 'col'), may hold values from -6 to 6
- diag_blocks: float32 [5, 32, 16, 128, 128], P(None, 'row', 'col'), may hold values from -1 to 2, as said below
- off_blocks: float32 [32, 16, 4, 8, 128, 128], P('row', 'col'), may hold values from -0.1875 to 0.1875
- slot_target: int32 [32, 16, 4, 8], P('row', 'col'), may hold values from 0 to 31
- slot_level: int32 [32, 16, 4, 8], P('row', 'col'), may hold values from 0 to 3, as said below
- slot_position: int32 [32, 16, 4, 8], P('row', 'col'), may hold values from 0 to 15
- slot_count: int32 [32, 16, 4], P('row', 'col'), may hold values from 1 to 8
Outputs:
- solution: float32 [5, 32, 16, 32, 128], P(None, 'row', 'col')
Inputs may be any that keep to these rules, and one draw needn't show every extreme that they name: slot_level[..., m, s] is a level below the target level m + 1. slot_target names a row group. slot_position names a column group. `diag_blocks`: each diagonal block is lower triangular with its diagonal between 1 and 2 and strictly lower entries of size at most 1 / sqrt(128).
All inputs are finite; a program needn't handle non-finite values.
Results may differ from a plain program's by a relative error of at most 0.0001.
Values sent between devices are 32-bit elements; how exact they have to be, the bound alone decides.
No kernel may reach another device: no remote copies, remote signals or barrier semaphores. Data moves between devices by JAX's collectives and lax.ppermute only.
A program may use at most 64 MiB of HBM per device.

v0:
```python
import jax
import jax.numpy as jnp
from jax import lax
from jax.sharding import PartitionSpec as P


def split_up(shard, dim, peers):
    before, after = (shard.shape[:dim], shard.shape[dim + 1 :])
    return jnp.moveaxis(shard.reshape(*before, peers, -1, *after), dim, 0)


def sum_at_owner(shard, axis, dim):
    peers = lax.axis_size(axis)
    tiles = lax.all_to_all(split_up(shard, dim, peers), axis, 0, 0, tiled=True)
    return jnp.sum(tiles, axis=0)


def from_everyone(shard, axis):
    peers = lax.axis_size(axis)
    return lax.all_to_all(
        jnp.broadcast_to(shard[None], (peers, *shard.shape)), axis, 0, 0, tiled=True
    )


def in_order(tiles, dim):
    dims = list(tiles.shape[1:])
    dims[dim] *= tiles.shape[0]
    return jnp.moveaxis(tiles, 0, dim).reshape(dims)


def gather_directly(shard, axis, dim):
    tiles = from_everyone(shard, axis)
    return in_order(tiles, dim)


def solve_block(diagonal, right_rows):
    return jax.scipy.linalg.solve_triangular(diagonal, right_rows.T, lower=True).T


def slot_products(gathered, blocks, source_ids, source_cols, weights):
    operands = gathered[source_ids, source_cols] * weights[:, None, None]
    return jnp.einsum("snb,sab->sna", operands, blocks, precision=lax.Precision.HIGHEST)


def per_device(
    right_side, diag_blocks, off_blocks, slot_target, slot_level, slot_position, slot_count
):
    right_rows = right_side[:, 0, 0]
    diagonal = diag_blocks[:, 0, 0]
    blocks = off_blocks[0, 0]
    targets = slot_target[0, 0]
    source_levels = slot_level[0, 0]
    positions = slot_position[0, 0]
    counts = slot_count[0, 0]
    level_total = right_rows.shape[0]
    width_rhs = right_rows.shape[1]
    slot_total = blocks.shape[1]
    col_count = lax.axis_size("col")
    gathered = jnp.zeros((level_total, col_count) + right_rows.shape[1:], jnp.float32)
    slot_ids = jnp.arange(slot_total, dtype=jnp.int32)
    solved = []
    pending = None
    for level_now in range(level_total):
        if level_now == 0:
            reduced = jnp.zeros(right_rows.shape[1:], jnp.float32)
        else:

            def partial_rows(
                begin_row, row_count, products=pending, target_now=targets[level_now - 1]
            ):
                first_block = begin_row // width_rhs
                block_count = row_count // width_rhs
                wanted = jnp.arange(block_count, dtype=jnp.int32)
                selector = (target_now[:, None] == wanted[None, :]).astype(jnp.float32)
                summed = jnp.einsum(
                    "st,sna->tna", selector, products, precision=lax.Precision.HIGHEST
                )
                return summed.reshape(block_count * width_rhs, summed.shape[2])

            reduced = sum_at_owner(
                partial_rows(jnp.int32(0), width_rhs * lax.axis_size("row")), "row", 0
            )
        current = solve_block(diagonal[level_now], right_rows[level_now] - reduced)
        solved.append(current)
        if level_now + 1 < level_total:
            source_ids = source_levels[level_now]
            source_cols = positions[level_now]
            active = slot_ids < counts[level_now]
            shared = gather_directly(current[None], "col", 0)
            gathered = gathered.at[level_now].set(shared)
            pending = slot_products(
                gathered, blocks[level_now], source_ids, source_cols, active.astype(jnp.float32)
            )
    return jnp.stack(solved)[:, None, None]


def solution(mesh):
    placed = (
        P(None, "row", "col", None, None),
        P(None, "row", "col", None, None),
        P("row", "col", None, None, None, None),
        P("row", "col", None, None),
        P("row", "col", None, None),
        P("row", "col", None, None),
        P("row", "col", None),
    )
    return jax.shard_map(
        per_device,
        mesh=mesh,
        in_specs=placed,
        out_specs=P(None, "row", "col", None, None),
        check_vma=False,
    )
```

profile of v0, /device:TPU:1, one launch (start us, length us, event | category | flops | bytes accessed | tf_op | source)
XLA Modules:
  0.0 226.1 jit_solution(7598081272775593265)
XLA Ops:
  0.0 1.7 fusion.26
  1.8 9.8 %custom-call.15 = f32[1,128,128]{1,2,0:T(8,128)S(1)} custom-call(f32[1,128,128]{2,1,0:T(8,128)S(1)} %get-tuple-element.57), custom_call_target="InvertDiagBlocksLowerTriangular" | custom-call | tf_op jit(solution)/shard_map/jit(_solve_triangular)/triangular_solve | solution.py:37
  13.8 15.9 %all-to-all-start = ((f32[16,1,32,128]{3,2,1,0:T(8,128)}), f32[16,1,32,128]{3,2,1,0:T(8,128)S(1)}, u32[]{:S(2)}, u32[]{:S(2)}) async-start(f32[16,1,32,128]{3,2,1,0:T(8,128)} %broadcast_in_dim.10), calls=%async_computation | async-start | bytes 524288 | tf_op jit(solution)/shard_map/all_to_all | solution.py:20
  32.1 11.3 %all-to-all-done = f32[16,1,32,128]{3,2,1,0:T(8,128)S(1)} async-done(((f32[16,1,32,128]{3,2,1,0:T(8,128)}), f32[16,1,32,128]{3,2,1,0:T(8,128)S(1)}, u32[]{:S(2)}, u32[]{:S(2)}) %all-to-all-start) | async-done | bytes 262176 | tf_op jit(solution)/shard_map/all_to_all | solution.py:20
  45.8 1.6 fusion.7
  49.6 12.7 %all-to-all-start.1 = ((f32[32,32,128]{2,1,0:T(8,128)}), f32[32,32,128]{2,1,0:T(8,128)}, u32[]{:S(2)}, u32[]{:S(2)}) async-start(f32[32,32,128]{2,1,0:T(8,128)} %copy.16), calls=%async_computation.1 | async-start | bytes 1048576 | tf_op jit(solution)/shard_map/all_to_all | solution.py:14
  62.3 10.6 %custom-call.16 = f32[1,128,128]{1,2,0:T(8,128)S(1)} custom-call(f32[1,128,128]{2,1,0:T(8,128)} %get-tuple-element.56), custom_call_target="InvertDiagBlocksLowerTriangular" | custom-call | tf_op jit(solution)/shard_map/jit(_solve_triangular)/triangular_solve | solution.py:37
  75.1 1.5 bitcast_dynamic-update-slice_fusion.5
  77.3 5.5 %all-to-all-start.2 = ((f32[16,1,32,128]{3,2,1,0:T(8,128)}), f32[16,1,32,128]{3,2,1,0:T(8,128)}, u32[]{:S(2)}, u32[]{:S(2)}) async-start(f32[16,1,32,128]{3,2,1,0:T(8,128)} %broadcast_in_dim.11), calls=%async_computation.2 | async-start | bytes 524288 | tf_op jit(solution)/shard_map/all_to_all | solution.py:20
  84.1 14.2 %all-to-all-done.2 = f32[16,1,32,128]{3,2,1,0:T(8,128)} async-done(((f32[16,1,32,128]{3,2,1,0:T(8,128)}), f32[16,1,32,128]{3,2,1,0:T(8,128)}, u32[]{:S(2)}, u32[]{:S(2)}) %all-to-all-start.2) | async-done | bytes 262176 | tf_op jit(solution)/shard_map/all_to_all | solution.py:20
  99.8 1.6 fusion.5
  102.9 9.9 %all-to-all-start.3 = ((f32[32,32,128]{2,1,0:T(8,128)}), f32[32,32,128]{2,1,0:T(8,128)}, u32[]{:S(2)}, u32[]{:S(2)}) async-start(f32[32,32,128]{2,1,0:T(8,128)} %copy.18), calls=%async_computation.3 | async-start | bytes 1048576 | tf_op jit(solution)/shard_map/all_to_all | solution.py:14
  112.9 10.6 %custom-call.17 = f32[1,128,128]{1,2,0:T(8,128)S(1)} custom-call(f32[1,128,128]{2,1,0:T(8,128)} %get-tuple-element.55), custom_call_target="InvertDiagBlocksLowerTriangular" | custom-call | tf_op jit(solution)/shard_map/jit(_solve_triangular)/triangular_solve | solution.py:37
  125.6 1.5 bitcast_dynamic-update-slice_fusion.4
  127.8 5.7 %all-to-all-start.4 = ((f32[16,1,32,128]{3,2,1,0:T(8,128)}), f32[16,1,32,128]{3,2,1,0:T(8,128)}, u32[]{:S(2)}, u32[]{:S(2)}) async-start(f32[16,1,32,128]{3,2,1,0:T(8,128)} %broadcast_in_dim.12), calls=%async_computation.4 | async-start | bytes 524288 | tf_op jit(solution)/shard_map/all_to_all | solution.py:20
  134.2 14.7 %all-to-all-done.4 = f32[16,1,32,128]{3,2,1,0:T(8,128)} async-done(((f32[16,1,32,128]{3,2,1,0:T(8,128)}), f32[16,1,32,128]{3,2,1,0:T(8,128)}, u32[]{:S(2)}, u32[]{:S(2)}) %all-to-all-start.4) | async-done | bytes 262176 | tf_op jit(solution)/shard_map/all_to_all | solution.py:20
  153.0 9.9 %all-to-all-start.5 = ((f32[32,32,128]{2,1,0:T(8,128)}), f32[32,32,128]{2,1,0:T(8,128)}, u32[]{:S(2)}, u32[]{:S(2)}) async-start(f32[32,32,128]{2,1,0:T(8,128)} %copy.20), calls=%async_computation.5 | async-start | bytes 1048576 | tf_op jit(solution)/shard_map/all_to_all | solution.py:14
  162.9 10.6 %custom-call.18 = f32[1,128,128]{1,2,0:T(8,128)S(1)} custom-call(f32[1,128,128]{2,1,0:T(8,128)} %get-tuple-element.58), custom_call_target="InvertDiagBlocksLowerTriangular" | custom-call | tf_op jit(solution)/shard_map/jit(_solve_triangular)/triangular_solve | solution.py:37
  175.7 1.5 bitcast_dynamic-update-slice_fusion.3
  177.9 5.7 %all-to-all-start.6 = ((f32[16,1,32,128]{3,2,1,0:T(8,128)}), f32[16,1,32,128]{3,2,1,0:T(8,128)}, u32[]{:S(2)}, u32[]{:S(2)}) async-start(f32[16,1,32,128]{3,2,1,0:T(8,128)} %broadcast_in_dim.13), calls=%async_computation.6 | async-start | bytes 524288 | tf_op jit(solution)/shard_map/all_to_all | solution.py:20
  184.3 14.7 %all-to-all-done.6 = f32[16,1,32,128]{3,2,1,0:T(8,128)} async-done(((f32[16,1,32,128]{3,2,1,0:T(8,128)}), f32[16,1,32,128]{3,2,1,0:T(8,128)}, u32[]{:S(2)}, u32[]{:S(2)}) %all-to-all-start.6) | async-done | bytes 262176 | tf_op jit(solution)/shard_map/all_to_all | solution.py:20
  203.1 9.9 %all-to-all-start.7 = ((f32[32,32,128]{2,1,0:T(8,128)}), f32[32,32,128]{2,1,0:T(8,128)S(1)}, u32[]{:S(2)}, u32[]{:S(2)}) async-start(f32[32,32,128]{2,1,0:T(8,128)} %copy.22), calls=%async_computation.7 | async-start | bytes 1048576 | tf_op jit(solution)/shard_map/all_to_all | solution.py:14
  213.0 10.6 %custom-call.19 = f32[1,128,128]{1,2,0:T(8,128)S(1)} custom-call(f32[1,128,128]{2,1,0:T(8,128)} %get-tuple-element.54), custom_call_target="InvertDiagBlocksLowerTriangular" | custom-call | tf_op jit(solution)/shard_map/jit(_solve_triangular)/triangular_solve | solution.py:37
  224.6 1.5 fusion
  (56 shorter events, 32.4 us)
Async XLA Ops:
  0.0 29.7 %copy-start.2 = (s32[1,1,4]{2,1,0:T(1,128)S(1)}, s32[1,1,4]{2,1,0:T(1,128)}, u32[]{:S(2)}) copy-start(s32[1,1,4]{2,1,0:T(1,128)} %param.23) | copy-start | bytes 52
  0.0 31.5 %copy-start.5 = (s32[1,1,4,8]{3,2,1,0:T(4,128)S(1)}, s32[1,1,4,8]{3,2,1,0:T(4,128)}, u32[]{:S(2)}) copy-start(s32[1,1,4,8]{3,2,1,0:T(4,128)} %param.20) | copy-start | bytes 388
  0.0 32.1 %copy-start.3 = (s32[1,1,4,8]{3,2,1,0:T(4,128)S(1)}, s32[1,1,4,8]{3,2,1,0:T(4,128)}, u32[]{:S(2)}) copy-start(s32[1,1,4,8]{3,2,1,0:T(4,128)} %param.22) | copy-start | bytes 388
  0.0 32.1 %copy-start.4 = (s32[1,1,4,8]{3,2,1,0:T(4,128)S(1)}, s32[1,1,4,8]{3,2,1,0:T(4,128)}, u32[]{:S(2)}) copy-start(s32[1,1,4,8]{3,2,1,0:T(4,128)} %param.21) | copy-start | bytes 388
  13.1 32.8 %copy-start = (f32[1,1,4,8,128,128]{5,4,3,2,1,0:T(8,128)S(1)}, f32[1,1,4,8,128,128]{5,4,3,2,1,0:T(8,128)}, u32[]{:S(2)}) copy-start(f32[1,1,4,8,128,128]{5,4,3,2,1,0:T(8,128)} %param.19) | copy-start | bytes 6291460
  13.8 29.6 %all-to-all-start = ((f32[16,1,32,128]{3,2,1,0:T(8,128)}), f32[16,1,32,128]{3,2,1,0:T(8,128)S(1)}, u32[]{:S(2)}, u32[]{:S(2)}) async-start(f32[16,1,32,128]{3,2,1,0:T(8,128)} %broadcast_in_dim.10), calls=%async_computation | async-start | bytes 524288 | tf_op jit(solution)/shard_map/all_to_all | solution.py:20
  43.4 0.7 copy-start.1
  49.6 24.4 %all-to-all-start.1 = ((f32[32,32,128]{2,1,0:T(8,128)}), f32[32,32,128]{2,1,0:T(8,128)}, u32[]{:S(2)}, u32[]{:S(2)}) async-start(f32[32,32,128]{2,1,0:T(8,128)} %copy.16), calls=%async_computation.1 | async-start | bytes 1048576 | tf_op jit(solution)/shard_map/all_to_all | solution.py:14
  75.1 26.3 %copy-start.8 = (s32[8]{0:T(128)S(1)}, s32[8]{0:T(128)}, u32[]{:S(2)}) copy-start(s32[8]{0:T(128)} %get-tuple-element.64) | copy-start | bytes 100
  77.3 20.9 %all-to-all-start.2 = ((f32[16,1,32,128]{3,2,1,0:T(8,128)}), f32[16,1,32,128]{3,2,1,0:T(8,128)}, u32[]{:S(2)}, u32[]{:S(2)}) async-start(f32[16,1,32,128]{3,2,1,0:T(8,128)} %broadcast_in_dim.11), calls=%async_computation.2 | async-start | bytes 524288 | tf_op jit(solution)/shard_map/all_to_all | solution.py:20
  102.9 21.6 %all-to-all-start.3 = ((f32[32,32,128]{2,1,0:T(8,128)}), f32[32,32,128]{2,1,0:T(8,128)}, u32[]{:S(2)}, u32[]{:S(2)}) async-start(f32[32,32,128]{2,1,0:T(8,128)} %copy.18), calls=%async_computation.3 | async-start | bytes 1048576 | tf_op jit(solution)/shard_map/all_to_all | solution.py:14
  125.6 25.8 %copy-start.7 = (s32[8]{0:T(128)S(1)}, s32[8]{0:T(128)}, u32[]{:S(2)}) copy-start(s32[8]{0:T(128)} %get-tuple-element.66) | copy-start | bytes 100
  127.8 21.1 %all-to-all-start.4 = ((f32[16,1,32,128]{3,2,1,0:T(8,128)}), f32[16,1,32,128]{3,2,1,0:T(8,128)}, u32[]{:S(2)}, u32[]{:S(2)}) async-start(f32[16,1,32,128]{3,2,1,0:T(8,128)} %broadcast_in_dim.12), calls=%async_computation.4 | async-start | bytes 524288 | tf_op jit(solution)/shard_map/all_to_all | solution.py:20
  153.0 21.6 %all-to-all-start.5 = ((f32[32,32,128]{2,1,0:T(8,128)}), f32[32,32,128]{2,1,0:T(8,128)}, u32[]{:S(2)}, u32[]{:S(2)}) async-start(f32[32,32,128]{2,1,0:T(8,128)} %copy.20), calls=%async_computation.5 | async-start | bytes 1048576 | tf_op jit(solution)/shard_map/all_to_all | solution.py:14
  175.7 25.8 %copy-start.6 = (s32[8]{0:T(128)S(1)}, s32[8]{0:T(128)}, u32[]{:S(2)}) copy-start(s32[8]{0:T(128)} %get-tuple-element.63) | copy-start | bytes 100
  177.9 21.1 %all-to-all-start.6 = ((f32[16,1,32,128]{3,2,1,0:T(8,128)}), f32[16,1,32,128]{3,2,1,0:T(8,128)}, u32[]{:S(2)}, u32[]{:S(2)}) async-start(f32[16,1,32,128]{3,2,1,0:T(8,128)} %broadcast_in_dim.13), calls=%async_computation.6 | async-start | bytes 524288 | tf_op jit(solution)/shard_map/all_to_all | solution.py:20
  203.1 21.5 %all-to-all-start.7 = ((f32[32,32,128]{2,1,0:T(8,128)}), f32[32,32,128]{2,1,0:T(8,128)S(1)}, u32[]{:S(2)}, u32[]{:S(2)}) async-start(f32[32,32,128]{2,1,0:T(8,128)} %copy.22), calls=%async_computation.7 | async-start | bytes 1048576 | tf_op jit(solution)/shard_map/all_to_all | solution.py:14
where the time goes:
time: 228 us; the launch traced here: 226 us
  starting transfers between devices  75.3 us (33%)
  other arithmetic  61.1 us (27%)
  waiting for transfers between devices  58.8 us (26%)
  local copies, waits for them, and re-layouts  15.5 us (7%)
  matrix products  15.1 us (7%)
    all_to_all x4, waiting for transfers between devices, from_everyone(): lax.all_to_all(jnp.broadcast_to(shard[None], (peers, *shard.shape)), axis...  54.9 us
    another operation x6, other arithmetic, solve_block(): jax.scipy.linalg.solve_triangular(diagonal, right_rows.T, lower=True)  54.1 us
    all_to_all x4, starting transfers between devices, sum_at_owner(): tiles = lax.all_to_all(split_up(shard, dim, peers), axis, 0, 0, tiled=True)  42.4 us
    all_to_all x4, starting transfers between devices, from_everyone(): lax.all_to_all(jnp.broadcast_to(shard[None], (peers, *shard.shape)), axis...  32.9 us
    another operation x5, matrix products, solve_block(): jax.scipy.linalg.solve_triangular(diagonal, right_rows.T, lower=True)  7.5 us
    dot_general x4, matrix products, slot_products(): jnp.einsum('snb,sab->sna', operands, blocks, precision=lax.Precision.HIGH...  5.12 us
  transfers between devices with their start and end apart: 8, of which 8 were waited for; matrix products, arithmetic and copies ran while one was open for 21% of the time, Pallas kernels for 0%

commit v1 on v0

v1 whole, which is shorter than its diff:
```python
import functools

import jax
import jax.numpy as jnp
from jax import lax
from jax.experimental import pallas as pl
from jax.experimental.pallas import tpu as pltpu
from jax.sharding import PartitionSpec as P

HIGHEST = lax.Precision.HIGHEST
VMEM = pltpu.VMEM
SMEM = pltpu.SMEM
BASE = 32


def mm(a, b):
    return jnp.dot(a, b, precision=HIGHEST, preferred_element_type=jnp.float32)


def mm_nt(a, b):
    return lax.dot_general(
        a, b, (((1,), (1,)), ((), ())), precision=HIGHEST, preferred_element_type=jnp.float32
    )


def invert_lower(blocks):
    size = blocks[0].shape[0]
    rows = lax.broadcasted_iota(jnp.int32, (size, size), 0)
    cols = lax.broadcasted_iota(jnp.int32, (size, size), 1)
    eye = rows == cols
    strict = rows > cols
    same = (rows // BASE) == (cols // BASE)
    scaled, scale_cols, powers, inverses = [], [], [], []
    for block in blocks:
        on_diag = jnp.where(eye, block, 0.0)
        scale_rows = 1.0 / jnp.sum(on_diag, axis=1, keepdims=True)
        scale_cols.append(1.0 / jnp.sum(on_diag, axis=0, keepdims=True))
        m = jnp.where(strict, block * scale_rows, 0.0)
        scaled.append(m)
        local = jnp.where(same, m, 0.0)
        powers.append(local)
        inverses.append(jnp.where(eye, 1.0, 0.0) - local)
    span = 2
    while span < BASE:
        powers = [mm(p, p) for p in powers]
        inverses = [v + mm(v, p) for v, p in zip(inverses, powers)]
        span *= 2
    width = BASE
    while width < size:
        joins = ((rows // (2 * width)) == (cols // (2 * width))) & (
            (rows // width) > (cols // width)
        )
        steps = [mm(jnp.where(joins, m, 0.0), v) for m, v in zip(scaled, inverses)]
        inverses = [v - mm(v, s) for v, s in zip(inverses, steps)]
        width *= 2
    return [v * s for v, s in zip(inverses, scale_cols)]


def first_kernel(diag_ref, right_ref, solved_ref, copies_ref):
    (inverse,) = invert_lower([diag_ref[...]])
    solved = mm_nt(right_ref[...], inverse)
    solved_ref[...] = solved
    for peer in range(copies_ref.shape[0]):
        copies_ref[peer] = solved


def invert_kernel(diag_ref, inverse_ref):
    count = diag_ref.shape[0]
    for at, inverse in enumerate(invert_lower([diag_ref[i] for i in range(count)])):
        inverse_ref[at] = inverse


def reduced_solve(received_ref, right_ref, inverse_ref):
    total = received_ref[0]
    for peer in range(1, received_ref.shape[0]):
        total = total + received_ref[peer]
    return mm_nt(right_ref[...] - total, inverse_ref[...])


def solve_kernel(received_ref, right_ref, inverse_ref, solved_ref, copies_ref):
    solved = reduced_solve(received_ref, right_ref, inverse_ref)
    solved_ref[...] = solved
    for peer in range(copies_ref.shape[0]):
        copies_ref[peer] = solved


def last_kernel(received_ref, right_ref, inverse_ref, *refs):
    earlier, out_ref = refs[:-1], refs[-1]
    for level, ref in enumerate(earlier):
        out_ref[level] = ref[...]
    out_ref[len(earlier)] = reduced_solve(received_ref, right_ref, inverse_ref)


def product_kernel(level, ids_ref, blocks_ref, *refs):
    gathered, out_ref = refs[:-1], refs[-1]
    slots = blocks_ref.shape[0]
    out_ref[...] = jnp.zeros_like(out_ref)
    count = ids_ref[3 * slots]
    products = []
    for s in range(slots):
        source_level = ids_ref[slots + s]
        position = ids_ref[2 * slots + s]
        operand = gathered[0][position]
        for other in range(1, level + 1):
            operand = jnp.where(source_level == other, gathered[other][position], operand)
        operand = jnp.where(s < count, operand, 0.0)
        products.append(mm_nt(operand, blocks_ref[s]))
    for s in range(slots):
        target = ids_ref[s]
        out_ref[target] = out_ref[target] + products[s]


def call(kernel, outs, in_spaces, flops, name):
    return pl.pallas_call(
        kernel,
        out_shape=outs,
        in_specs=[pl.BlockSpec(memory_space=space) for space in in_spaces],
        out_specs=jax.tree.map(lambda _: pl.BlockSpec(memory_space=VMEM), outs),
        cost_estimate=pl.CostEstimate(flops=flops, bytes_accessed=1 << 20, transcendentals=0),
        compiler_params=pltpu.CompilerParams(vmem_limit_bytes=16 << 20),
        name=name,
    )


def per_device(
    right_side, diag_blocks, off_blocks, slot_target, slot_level, slot_position, slot_count
):
    right_rows = right_side[:, 0, 0]
    diagonal = diag_blocks[:, 0, 0]
    blocks = off_blocks[0, 0]
    level_total, width_rhs, width = right_rows.shape
    row_peers = lax.axis_size("row")
    col_peers = lax.axis_size("col")
    f32 = jnp.float32
    solved_shape = jax.ShapeDtypeStruct((width_rhs, width), f32)
    copies_shape = jax.ShapeDtypeStruct((col_peers, width_rhs, width), f32)
    partial_shape = jax.ShapeDtypeStruct((row_peers, width_rhs, width), f32)
    out_shape = jax.ShapeDtypeStruct((level_total, width_rhs, width), f32)
    counts = jnp.broadcast_to(slot_count[0, 0][:, None], slot_target.shape[2:])
    ids = jnp.concatenate(
        [slot_target[0, 0], slot_level[0, 0], slot_position[0, 0], counts], axis=1
    )

    solved, copies = call(
        first_kernel, (solved_shape, copies_shape), (VMEM, VMEM), 1 << 26, "first"
    )(diagonal[0], right_rows[0])
    inverses = call(
        invert_kernel,
        jax.ShapeDtypeStruct((level_total - 1, width, width), f32),
        (VMEM,),
        1 << 28,
        "invert",
    )(diagonal[1:])
    results, gathered = [solved], []
    for level in range(level_total - 1):
        gathered.append(lax.all_to_all(copies, "col", 0, 0, tiled=True))
        partial = call(
            functools.partial(product_kernel, level),
            partial_shape,
            (SMEM,) + (VMEM,) * (level + 2),
            1 << 26,
            "products",
        )(ids[level], blocks[level], *gathered)
        received = lax.all_to_all(partial, "row", 0, 0, tiled=True)
        if level + 2 < level_total:
            solved, copies = call(
                solve_kernel, (solved_shape, copies_shape), (VMEM,) * 3, 1 << 24, "solve"
            )(received, right_rows[level + 1], inverses[level])
            results.append(solved)
        else:
            out = call(last_kernel, out_shape, (VMEM,) * (3 + len(results)), 1 << 24, "last")(
                received, right_rows[level + 1], inverses[level], *results
            )
    return out[:, None, None]


def solution(mesh):
    placed = (
        P(None, "row", "col", None, None),
        P(None, "row", "col", None, None),
        P("row", "col", None, None, None, None),
        P("row", "col", None, None),
        P("row", "col", None, None),
        P("row", "col", None, None),
        P("row", "col", None),
    )
    return jax.shard_map(
        per_device,
        mesh=mesh,
        in_specs=placed,
        out_specs=P(None, "row", "col", None, None),
        check_vma=False,
    )
```

time: 228 us -> 186 us (0.82)
  blocking collectives: 0 us -> 118 us
  other arithmetic: 61.1 us -> 0.79 us
  starting transfers between devices: 75.3 us -> 28.4 us
  waiting for transfers between devices: 58.8 us -> 18.9 us
  matrix products: 15.1 us -> 0 us
  Pallas kernels: 0 us -> 14.6 us
  local copies, waits for them, and re-layouts: 15.5 us -> 4.09 us
    all_to_all x0 -> x6, blocking collectives: none -> 118 us  [the longest x3 62.2 us: per_device(): gathered.append(lax.all_to_all(copies, 'col', 0, 0, tiled=True))]
    another operation x6 -> x0, other arithmetic: 54.1 us -> none  [solve_block(): jax.scipy.linalg.solve_triangular(diagonal, right_rows.T, lower=True)]
    all_to_all x8 -> x2, starting transfers between devices: 75.3 us -> 28.4 us  [the longest x1 15.7 us: per_device(): gathered.append(lax.all_to_all(copies, 'col', 0, 0, tiled=True))]
    all_to_all x8 -> x2, waiting for transfers between devices: 58.8 us -> 18.9 us  [the longest x1 10.6 us: per_device(): gathered.append(lax.all_to_all(copies, 'col', 0, 0, tiled=True))]
    pallas_call x0 -> x10, Pallas kernels: none -> 14.6 us  [the longest x4 6.72 us: per_device(): call(functools.partial(product_kernel, level), partial_shape, (SMEM,) + (...]
    dot_general x8 -> x0, matrix products: 7.64 us -> none  [the longest x4 5.12 us: slot_products(): jnp.einsum('snb,sab->sna', operands, blocks, precision=lax.Precision.HIGH...]
    another operation x5 -> x0, matrix products: 7.5 us -> none  [solve_block(): jax.scipy.linalg.solve_triangular(diagonal, right_rows.T, lower=True)]
    dot_general x4 -> x0, local copies, waits for them, and re-layouts: 4.4 us -> none  [partial_rows(): jnp.einsum('st,sna->tna', selector, products, precision=lax.Precision.HIG...]
  transfers between devices with their start and end apart: 8 -> 2, of which waited for: 8 -> 2; matrix products, arithmetic and copies ran while one was open for 21% -> 2% of each run, Pallas kernels for 0% -> 2%
where the time goes in v1:
time: 186 us; the launch traced here: 185 us
  blocking collectives  118 us (63%)
  starting transfers between devices  28.4 us (15%)
  waiting for transfers between devices  18.9 us (10%)
  Pallas kernels  14.6 us (8%)
  local copies, waits for them, and re-layouts  4.09 us (2%)
    all_to_all x3, blocking collectives, per_device(): gathered.append(lax.all_to_all(copies, 'col', 0, 0, tiled=True))  62.2 us
    all_to_all x3, blocking collectives, per_device(): received = lax.all_to_all(partial, 'row', 0, 0, tiled=True)  55.8 us
    all_to_all x1, starting transfers between devices, per_device(): gathered.append(lax.all_to_all(copies, 'col', 0, 0, tiled=True))  15.7 us
    all_to_all x1, starting transfers between devices, per_device(): received = lax.all_to_all(partial, 'row', 0, 0, tiled=True)  12.6 us
    all_to_all x1, waiting for transfers between devices, per_device(): gathered.append(lax.all_to_all(copies, 'col', 0, 0, tiled=True))  10.6 us
    all_to_all x1, waiting for transfers between devices, per_device(): received = lax.all_to_all(partial, 'row', 0, 0, tiled=True)  8.33 us
    pallas_call x4, Pallas kernels, per_device(): call(functools.partial(product_kernel, level), partial_shape, (SMEM,) + (...  6.72 us
  transfers between devices with their start and end apart: 2, of which 2 were waited for; matrix products, arithmetic and copies ran while one was open for 2% of the time, Pallas kernels for 2%

profile of v1, /device:TPU:1, one launch (start us, length us, event | category | flops | bytes accessed | tf_op | source)
XLA Modules:
  0.0 184.8 jit_solution(3868748696345220990)
XLA Ops:
  0.0 0.8 slice_bitcast_fusion.10
  0.8 0.8 slice_bitcast_fusion.9.diag_ref
  1.6 3.1 %first.1 = (f32[32,128]{1,0:T(8,128)S(1)}, f32[16,32,128]{2,1,0:T(8,128)}) custom-call(f32[128,128]{1,0:T(8,128)S(1)} %slice_bitcast_fusion.9.diag_ref, f32[32,128]{1,0:T(8,128)S(1)} %get-tuple-element.32.right_ref), custom_call_target="tpu_custom_call" | custom-call | flops 67108864 | bytes 1048576 | tf_op jit(solution)/shard_map/first/pallas_call | solution.py:144
  4.7 15.7 %all-to-all-start = ((f32[16,32,128]{2,1,0:T(8,128)}), f32[16,32,128]{2,1,0:T(8,128)S(1)}, u32[]{:S(2)}, u32[]{:S(2)}) async-start(f32[16,32,128]{2,1,0:T(8,128)} %get-tuple-element.13), calls=%async_computation | async-start | bytes 524288 | tf_op jit(solution)/shard_map/all_to_all | solution.py:156
  20.5 0.7 broadcast_in_dim.11
  21.2 0.8 pad_add_fusion
  22.0 1.7 slice_bitcast_fusion
  23.7 10.6 %all-to-all-done.refs_0_ = f32[16,32,128]{2,1,0:T(8,128)S(1)} async-done(((f32[16,32,128]{2,1,0:T(8,128)}), f32[16,32,128]{2,1,0:T(8,128)S(1)}, u32[]{:S(2)}, u32[]{:S(2)}) %all-to-all-start) | async-done | bytes 262176 | tf_op jit(solution)/shard_map/all_to_all | solution.py:156
  34.2 2.3 %products.4 = f32[32,32,128]{2,1,0:T(8,128)} custom-call(s32[32]{0:T(128)S(1)} %get-tuple-element.36.ids_ref, f32[8,128,128]{2,1,0:T(8,128)S(1)} %get-tuple-element.22.blocks_ref, f32[16,32,128]{2,1,0:T(8,128)S(1)} %all-to-all-done.refs_0_), custom_call_target="tpu_custom_call" | custom-call | flops 67108864 | bytes 1048576 | tf_op jit(solution)/shard_map/products/pallas_call | solution.py:157
  36.5 12.6 %all-to-all-start.1 = ((f32[32,32,128]{2,1,0:T(8,128)}), f32[32,32,128]{2,1,0:T(8,128)S(1)}, u32[]{:S(2)}, u32[]{:S(2)}) async-start(f32[32,32,128]{2,1,0:T(8,128)} %products.4), calls=%async_computation.1 | async-start | bytes 1048576 | tf_op jit(solution)/shard_map/all_to_all | solution.py:164
  49.2 3.2 %invert.1 = f32[4,128,128]{2,1,0:T(8,128)S(1)} custom-call(f32[4,128,128]{2,1,0:T(8,128)S(1)} %slice_bitcast_fusion.4.diag_ref), custom_call_target="tpu_custom_call" | custom-call | flops 268435456 | bytes 1048576 | tf_op jit(solution)/shard_map/invert/pallas_call | solution.py:147
  52.4 8.3 %all-to-all-done.1.received_ref = f32[32,32,128]{2,1,0:T(8,128)S(1)} async-done(((f32[32,32,128]{2,1,0:T(8,128)}), f32[32,32,128]{2,1,0:T(8,128)S(1)}, u32[]{:S(2)}, u32[]{:S(2)}) %all-to-all-start.1) | async-done | bytes 524320 | tf_op jit(solution)/shard_map/all_to_all | solution.py:164
  61.0 20.6 %all_to_all.40.refs_1_ = f32[16,32,128]{2,1,0:T(8,128)S(1)} all-to-all(f32[16,32,128]{2,1,0:T(8,128)S(1)} %get-tuple-element.14), channel_id=1, replica_groups=mesh['row'=32,'col'=16] {'col'}, dimensions={0} | all-to-all | bytes 524288 | tf_op jit(solution)/shard_map/all_to_all | solution.py:156
  81.6 1.5 products.5
  83.1 18.6 %all_to_all.41.received_ref = f32[32,32,128]{2,1,0:T(8,128)S(1)} all-to-all(f32[32,32,128]{2,1,0:T(8,128)S(1)} %products.5), channel_id=1, replica_groups=mesh['row'=32,'col'=16] {'row'}, dimensions={0} | all-to-all | bytes 1048576 | tf_op jit(solution)/shard_map/all_to_all | solution.py:164
  101.7 0.2 solve.4
  102.0 20.8 %all_to_all.42.refs_2_ = f32[16,32,128]{2,1,0:T(8,128)S(1)} all-to-all(f32[16,32,128]{2,1,0:T(8,128)S(1)} %get-tuple-element.15), channel_id=1, replica_groups=mesh['row'=32,'col'=16] {'col'}, dimensions={0} | all-to-all | bytes 524288 | tf_op jit(solution)/shard_map/all_to_all | solution.py:156
  122.8 1.5 products.6
  124.2 18.6 %all_to_all.43.received_ref = f32[32,32,128]{2,1,0:T(8,128)S(1)} all-to-all(f32[32,32,128]{2,1,0:T(8,128)S(1)} %products.6), channel_id=1, replica_groups=mesh['row'=32,'col'=16] {'row'}, dimensions={0} | all-to-all | bytes 1048576 | tf_op jit(solution)/shard_map/all_to_all | solution.py:164
  142.8 0.2 solve.5
  143.1 20.8 %all_to_all.44.refs_3_ = f32[16,32,128]{2,1,0:T(8,128)S(1)} all-to-all(f32[16,32,128]{2,1,0:T(8,128)S(1)} %get-tuple-element.16), channel_id=1, replica_groups=mesh['row'=32,'col'=16] {'col'}, dimensions={0} | all-to-all | bytes 524288 | tf_op jit(solution)/shard_map/all_to_all | solution.py:156
  163.9 1.5 products.7
  165.3 18.6 %all_to_all.45.received_ref = f32[32,32,128]{2,1,0:T(8,128)S(1)} all-to-all(f32[32,32,128]{2,1,0:T(8,128)S(1)} %products.7), channel_id=1, replica_groups=mesh['row'=32,'col'=16] {'row'}, dimensions={0} | all-to-all | bytes 1048576 | tf_op jit(solution)/shard_map/all_to_all | solution.py:164
  183.9 0.9 last.1
  (6 shorter events, 0.3 us)
Async XLA Ops:
  4.7 29.5 %all-to-all-start = ((f32[16,32,128]{2,1,0:T(8,128)}), f32[16,32,128]{2,1,0:T(8,128)S(1)}, u32[]{:S(2)}, u32[]{:S(2)}) async-start(f32[16,32,128]{2,1,0:T(8,128)} %get-tuple-element.13), calls=%async_computation | async-start | bytes 524288 | tf_op jit(solution)/shard_map/all_to_all | solution.py:156
  23.7 25.5 %copy-start = (f32[5,1,1,128,128]{4,3,2,1,0:T(8,128)S(1)}, f32[5,1,1,128,128]{4,3,2,1,0:T(8,128)}, u32[]{:S(2)}) copy-start(f32[5,1,1,128,128]{4,3,2,1,0:T(8,128)} %param.8) | copy-start | bytes 983044
  36.5 24.3 %all-to-all-start.1 = ((f32[32,32,128]{2,1,0:T(8,128)}), f32[32,32,128]{2,1,0:T(8,128)S(1)}, u32[]{:S(2)}, u32[]{:S(2)}) async-start(f32[32,32,128]{2,1,0:T(8,128)} %products.4), calls=%async_computation.1 | async-start | bytes 1048576 | tf_op jit(solution)/shard_map/all_to_all | solution.py:164

commit v2 on v1

v2 whole, which is shorter than its diff:
```python
import functools

import jax
import jax.numpy as jnp
from jax import lax
from jax.experimental import pallas as pl
from jax.experimental.pallas import tpu as pltpu
from jax.sharding import Mesh
from jax.sharding import PartitionSpec as P

HIGHEST = lax.Precision.HIGHEST
VMEM = pltpu.VMEM
BASE = 32
GRANT = 16 << 20


def mm(a, b):
    return jnp.dot(a, b, precision=HIGHEST, preferred_element_type=jnp.float32)


def mm_nt(a, b):
    return lax.dot_general(
        a, b, (((1,), (1,)), ((), ())), precision=HIGHEST, preferred_element_type=jnp.float32
    )


def invert_lower(blocks):
    size = blocks[0].shape[0]
    rows = lax.broadcasted_iota(jnp.int32, (size, size), 0)
    cols = lax.broadcasted_iota(jnp.int32, (size, size), 1)
    eye = rows == cols
    strict = rows > cols
    same = (rows // BASE) == (cols // BASE)
    scaled, scale_cols, powers, inverses = [], [], [], []
    for block in blocks:
        on_diag = jnp.where(eye, block, 0.0)
        scale_rows = 1.0 / jnp.sum(on_diag, axis=1, keepdims=True)
        scale_cols.append(1.0 / jnp.sum(on_diag, axis=0, keepdims=True))
        m = jnp.where(strict, block * scale_rows, 0.0)
        scaled.append(m)
        local = jnp.where(same, m, 0.0)
        powers.append(local)
        inverses.append(jnp.where(eye, 1.0, 0.0) - local)
    span = 2
    while span < BASE:
        powers = [mm(p, p) for p in powers]
        inverses = [v + mm(v, p) for v, p in zip(inverses, powers)]
        span *= 2
    width = BASE
    while width < size:
        joins = ((rows // (2 * width)) == (cols // (2 * width))) & (
            (rows // width) > (cols // width)
        )
        steps = [mm(jnp.where(joins, m, 0.0), v) for m, v in zip(scaled, inverses)]
        inverses = [v - mm(v, s) for v, s in zip(inverses, steps)]
        width *= 2
    return [v * s for v, s in zip(inverses, scale_cols)]


def first_kernel(*refs):
    diag_hbm, right_hbm = refs[:2]
    inverse_ref, solved_ref, copies_ref = refs[7:10]
    kept_refs = refs[10:16]
    diag_ref, sems = refs[16:]
    moves = [pltpu.make_async_copy(diag_hbm, diag_ref, sems.at[0])]
    for at, (source, kept) in enumerate(zip(refs[1:7], kept_refs)):
        moves.append(pltpu.make_async_copy(source, kept, sems.at[at + 1]))
    for move in moves:
        move.start()
    moves[0].wait()
    moves[1].wait()
    level_total = diag_ref.shape[0]
    inverses = invert_lower([diag_ref[level, 0, 0] for level in range(level_total)])
    solved = mm_nt(kept_refs[0][0, 0, 0], inverses[0])
    solved_ref[...] = solved
    for peer in range(copies_ref.shape[0]):
        copies_ref[peer] = solved
    for level in range(1, level_total):
        inverse_ref[level - 1] = inverses[level]
    for move in moves[2:]:
        move.wait()


def reduced_solve(level, received_ref, right_ref, inverse_ref):
    total = received_ref[0]
    for peer in range(1, received_ref.shape[0]):
        total = total + received_ref[peer]
    return mm_nt(right_ref[level, 0, 0] - total, inverse_ref[level - 1])


def solve_kernel(level, received_ref, right_ref, inverse_ref, solved_ref, copies_ref):
    solved = reduced_solve(level, received_ref, right_ref, inverse_ref)
    solved_ref[...] = solved
    for peer in range(copies_ref.shape[0]):
        copies_ref[peer] = solved


def last_kernel(received_ref, right_ref, inverse_ref, *refs):
    earlier, out_ref = refs[:-1], refs[-1]
    for level, ref in enumerate(earlier):
        out_ref[level] = ref[...]
    level = len(earlier)
    out_ref[level] = reduced_solve(level, received_ref, right_ref, inverse_ref)


def split(value):
    high = value.astype(jnp.bfloat16)
    return high, (value - high.astype(jnp.float32)).astype(jnp.bfloat16)


def product(operand, block):
    rows = operand.shape[0]
    operand_high, operand_low = split(operand)
    block_high, block_low = split(block)
    contract = (((1,), (1,)), ((), ()))
    both = lax.dot_general(
        jnp.concatenate([operand_high, operand_low], axis=0),
        block_high,
        contract,
        preferred_element_type=jnp.float32,
    )
    rest = lax.dot_general(
        operand_high, block_low, contract, preferred_element_type=jnp.float32
    )
    return both[:rows] + (both[rows:] + rest)


def product_kernel(tier, target_ref, level_ref, position_ref, count_ref, blocks_ref, *refs):
    gathered, out_ref = refs[:-1], refs[-1]
    slots = blocks_ref.shape[3]
    out_ref[...] = jnp.zeros_like(out_ref)
    targets, source_levels = target_ref[0, 0, tier], level_ref[0, 0, tier]
    positions, count = position_ref[0, 0, tier], count_ref[0, 0][tier]
    products = []
    for s in range(slots):
        position = positions[s]
        near, far = position % 2, position // 2
        operand = gathered[0][near, far]
        for other in range(1, tier + 1):
            operand = jnp.where(source_levels[s] == other, gathered[other][near, far], operand)
        operand = jnp.where(s < count, operand, 0.0)
        products.append(product(operand, blocks_ref[0, 0, tier, s]))
    for s in range(slots):
        target = targets[s]
        out_ref[target] = out_ref[target] + products[s]


def call(kernel, outs, in_spaces, name, scratch=(), grant=16 << 20):
    return pl.pallas_call(
        kernel,
        out_shape=outs,
        in_specs=[pl.BlockSpec(memory_space=space) for space in in_spaces],
        out_specs=jax.tree.map(lambda _: pl.BlockSpec(memory_space=VMEM), outs),
        cost_estimate=pl.CostEstimate(flops=1 << 26, bytes_accessed=1 << 20, transcendentals=0),
        scratch_shapes=scratch,
        compiler_params=pltpu.CompilerParams(vmem_limit_bytes=grant),
        name=name,
    )


def collect(copies):
    strided = lax.all_to_all(copies, "far", 0, 0, tiled=True)
    return lax.all_gather(strided, "near", axis=0, tiled=False)


def per_device(
    right_side, diag_blocks, off_blocks, slot_target, slot_level, slot_position, slot_count
):
    level_total = right_side.shape[0]
    block = right_side.shape[3:]
    width = block[1]
    row_peers = lax.axis_size("chip") * lax.axis_size("core")
    f32 = jnp.float32
    solved_shape = jax.ShapeDtypeStruct(block, f32)
    copies_shape = jax.ShapeDtypeStruct((lax.axis_size("far"), *block), f32)
    partial_shape = jax.ShapeDtypeStruct((row_peers, *block), f32)
    out_shape = jax.ShapeDtypeStruct((level_total, *block), f32)
    inverse_shape = jax.ShapeDtypeStruct((level_total - 1, width, width), f32)

    kept = (right_side, off_blocks, slot_target, slot_level, slot_position, slot_count)
    kept_shapes = tuple(jax.ShapeDtypeStruct(array.shape, array.dtype) for array in kept)
    inverses, solved, copies, *kept = call(
        first_kernel,
        (inverse_shape, solved_shape, copies_shape, *kept_shapes),
        (pltpu.HBM,) * 7,
        "first",
        (pltpu.VMEM(diag_blocks.shape, f32), pltpu.SemaphoreType.DMA((7,))),
        GRANT,
    )(*(pltpu.with_memory_space_constraint(x, pltpu.HBM) for x in (diag_blocks, *kept)))
    right_side, off_blocks, *slot_tables = kept
    results, gathered = [solved], []
    for level in range(1, level_total):
        gathered.append(collect(copies))
        partial = call(
            functools.partial(product_kernel, level - 1),
            partial_shape,
            (VMEM,) * (level + 5),
            "products",
        )(*slot_tables, off_blocks, *gathered)
        received = lax.all_to_all(partial, ("chip", "core"), 0, 0, tiled=True)
        if level + 1 < level_total:
            solved, copies = call(
                functools.partial(solve_kernel, level),
                (solved_shape, copies_shape),
                (VMEM,) * 3,
                "solve",
            )(received, right_side, inverses)
            results.append(solved)
        else:
            out = call(last_kernel, out_shape, (VMEM,) * (3 + len(results)), "last")(
                received, right_side, inverses, *results
            )
    return out[:, None, None]


def solution(mesh):
    rows, cols = mesh.shape["row"], mesh.shape["col"]
    fine = Mesh(
        mesh.devices.reshape(rows // 2, 2, cols // 2, 2), ("chip", "core", "far", "near")
    )
    row, col = ("chip", "core"), ("far", "near")
    placed = (
        P(None, row, col, None, None),
        P(None, row, col, None, None),
        P(row, col, None, None, None, None),
        P(row, col, None, None),
        P(row, col, None, None),
        P(row, col, None, None),
        P(row, col, None),
    )
    return jax.shard_map(
        per_device,
        mesh=fine,
        in_specs=placed,
        out_specs=P(None, row, col, None, None),
        check_vma=False,
    )
```

time: 186 us -> 184 us (0.989)
  blocking collectives: 118 us -> 176 us
  starting transfers between devices: 28.4 us -> 0 us
  waiting for transfers between devices: 18.9 us -> 0 us
  Pallas kernels: 14.6 us -> 8.31 us
  local copies, waits for them, and re-layouts: 4.09 us -> 0 us
    all_to_all x6 -> x8, blocking collectives: 118 us -> 155 us  [the longest x4 84 us: collect(): strided = lax.all_to_all(copies, 'far', 0, 0, tiled=True)]
    all_to_all x2 -> x0, starting transfers between devices: 28.4 us -> none  [the longest x1 15.7 us: per_device(): gathered.append(lax.all_to_all(copies, 'col', 0, 0, tiled=True))]
    all_gather x0 -> x4, blocking collectives: none -> 20.3 us  [collect(): return lax.all_gather(strided, 'near', axis=0, tiled=False)]
    all_to_all x2 -> x0, waiting for transfers between devices: 18.9 us -> none  [the longest x1 10.6 us: per_device(): gathered.append(lax.all_to_all(copies, 'col', 0, 0, tiled=True))]
    pallas_call x10 -> x9, Pallas kernels: 14.6 us -> 8.31 us  [the longest x1 4.79 us: per_device(): call(first_kernel, (inverse_shape, solved_shape, copies_shape, *kept_shap...]
    squeeze x5 -> x0, local copies, waits for them, and re-layouts: 3.34 us -> none  [the longest x1 1.68 us: per_device(): blocks[level]]
  transfers between devices with their start and end apart: 2 -> 0, of which waited for: 2 -> 0; matrix products, arithmetic and copies ran while one was open for 2% -> 0% of each run, Pallas kernels for 2% -> 0%
where the time goes in v2:
time: 184 us
  blocking collectives  176 us (96%)
  Pallas kernels  8.31 us (5%)
    all_to_all x4, blocking collectives, collect(): strided = lax.all_to_all(copies, 'far', 0, 0, tiled=True)  84 us
    all_to_all x4, blocking collectives, per_device(): received = lax.all_to_all(partial, ('chip', 'core'), 0, 0, tiled=True)  71.3 us
    all_gather x4, blocking collectives, collect(): return lax.all_gather(strided, 'near', axis=0, tiled=False)  20.3 us
    pallas_call x1, Pallas kernels, per_device(): call(first_kernel, (inverse_shape, solved_shape, copies_shape, *kept_shap...  4.79 us

profile of v2, /device:TPU:1, one launch (start us, length us, event | category | flops | bytes accessed | tf_op | source)
XLA Modules:
  0.0 184.0 jit_solution(17015939058881980632)
XLA Ops:
  0.0 4.8 %first.1 = (f32[4,128,128]{2,1,0:T(8,128)S(1)}, f32[32,128]{1,0:T(8,128)S(1)}, f32[8,32,128]{2,1,0:T(8,128)S(1)}, f32[5,1,1,32,128]{4,3,2,1,0:T(8,128)S(1)}, f32...) custom-call(f32[5,1,1,128,128]{4,3,2,1,0:T(8,128)} %refs_0_.1, ...), custom_call_target="tpu_custom_call" | custom-call | flops 67108864 | bytes 1048576 | tf_op jit(solution)/shard_map/first/pallas_call | solution.py:182
  4.8 28.6 %all_to_all.40 = f32[8,32,128]{2,1,0:T(8,128)S(1)} all-to-all(f32[8,32,128]{2,1,0:T(8,128)S(1)} %get-tuple-element.25), channel_id=1, replica_groups=mesh['chip'=16,'core'=2,'far'=8,'near'=2] {'far'}, dimensions={0} | all-to-all | bytes 262144 | tf_op jit(solution)/shard_map/all_to_all | solution.py:162
  33.4 4.5 %all-gather = f32[16,32,128]{2,1,0:T(8,128)S(1)} all-gather(f32[8,32,128]{2,1,0:T(8,128)S(1)} %all_to_all.40), channel_id=2, replica_groups=mesh['chip'=16,'core'=2,'far'=8,'near'=2] {'near'}, dimensions={0}, use_global_device_ids=true | all-gather | bytes 393216 | tf_op jit(solution)/shard_map/all_gather | solution.py:163
  37.9 0.5 products.4
  38.4 23.4 %all_to_all.41.received_ref = f32[32,32,128]{2,1,0:T(8,128)S(1)} all-to-all(f32[32,32,128]{2,1,0:T(8,128)S(1)} %products.4), channel_id=1, replica_groups=mesh['chip'=16,'core'=2,'far'=8,'near'=2] {'chip','core'}, dimensions={0} | all-to-all | bytes 1048576 | tf_op jit(solution)/shard_map/all_to_all | solution.py:200
  61.8 0.2 solve.3
  62.0 18.7 %all_to_all.42 = f32[8,32,128]{2,1,0:T(8,128)S(1)} all-to-all(f32[8,32,128]{2,1,0:T(8,128)S(1)} %get-tuple-element.28), channel_id=1, replica_groups=mesh['chip'=16,'core'=2,'far'=8,'near'=2] {'far'}, dimensions={0} | all-to-all | bytes 262144 | tf_op jit(solution)/shard_map/all_to_all | solution.py:162
  80.7 5.3 %all-gather.1 = f32[16,32,128]{2,1,0:T(8,128)S(1)} all-gather(f32[8,32,128]{2,1,0:T(8,128)S(1)} %all_to_all.42), channel_id=3, replica_groups=mesh['chip'=16,'core'=2,'far'=8,'near'=2] {'near'}, dimensions={0}, use_global_device_ids=true | all-gather | bytes 393216 | tf_op jit(solution)/shard_map/all_gather | solution.py:163
  86.0 0.5 products.5
  86.5 16.1 %all_to_all.43.received_ref = f32[32,32,128]{2,1,0:T(8,128)S(1)} all-to-all(f32[32,32,128]{2,1,0:T(8,128)S(1)} %products.5), channel_id=1, replica_groups=mesh['chip'=16,'core'=2,'far'=8,'near'=2] {'chip','core'}, dimensions={0} | all-to-all | bytes 1048576 | tf_op jit(solution)/shard_map/all_to_all | solution.py:200
  102.5 0.2 solve.4
  102.8 18.2 %all_to_all.44 = f32[8,32,128]{2,1,0:T(8,128)S(1)} all-to-all(f32[8,32,128]{2,1,0:T(8,128)S(1)} %get-tuple-element.29), channel_id=1, replica_groups=mesh['chip'=16,'core'=2,'far'=8,'near'=2] {'far'}, dimensions={0} | all-to-all | bytes 262144 | tf_op jit(solution)/shard_map/all_to_all | solution.py:162
  121.0 5.3 %all-gather.2 = f32[16,32,128]{2,1,0:T(8,128)S(1)} all-gather(f32[8,32,128]{2,1,0:T(8,128)S(1)} %all_to_all.44), channel_id=4, replica_groups=mesh['chip'=16,'core'=2,'far'=8,'near'=2] {'near'}, dimensions={0}, use_global_device_ids=true | all-gather | bytes 393216 | tf_op jit(solution)/shard_map/all_gather | solution.py:163
  126.3 0.5 products.6
  126.8 15.8 %all_to_all.45.received_ref = f32[32,32,128]{2,1,0:T(8,128)S(1)} all-to-all(f32[32,32,128]{2,1,0:T(8,128)S(1)} %products.6), channel_id=1, replica_groups=mesh['chip'=16,'core'=2,'far'=8,'near'=2] {'chip','core'}, dimensions={0} | all-to-all | bytes 1048576 | tf_op jit(solution)/shard_map/all_to_all | solution.py:200
  142.6 0.2 solve.5
  142.9 18.5 %all_to_all.46 = f32[8,32,128]{2,1,0:T(8,128)S(1)} all-to-all(f32[8,32,128]{2,1,0:T(8,128)S(1)} %get-tuple-element.30), channel_id=1, replica_groups=mesh['chip'=16,'core'=2,'far'=8,'near'=2] {'far'}, dimensions={0} | all-to-all | bytes 262144 | tf_op jit(solution)/shard_map/all_to_all | solution.py:162
  161.3 5.3 %all-gather.3 = f32[16,32,128]{2,1,0:T(8,128)S(1)} all-gather(f32[8,32,128]{2,1,0:T(8,128)S(1)} %all_to_all.46), channel_id=5, replica_groups=mesh['chip'=16,'core'=2,'far'=8,'near'=2] {'near'}, dimensions={0}, use_global_device_ids=true | all-gather | bytes 393216 | tf_op jit(solution)/shard_map/all_gather | solution.py:163
  166.6 0.5 products.7
  167.1 16.0 %all_to_all.47.received_ref = f32[32,32,128]{2,1,0:T(8,128)S(1)} all-to-all(f32[32,32,128]{2,1,0:T(8,128)S(1)} %products.7), channel_id=1, replica_groups=mesh['chip'=16,'core'=2,'far'=8,'near'=2] {'chip','core'}, dimensions={0} | all-to-all | bytes 1048576 | tf_op jit(solution)/shard_map/all_to_all | solution.py:200
  183.1 0.9 last.1

commit v3 on v2

--- a/solution.py
+++ b/solution.py
@@ -126,23 +126,25 @@
 
 
 def product_kernel(tier, target_ref, level_ref, position_ref, count_ref, blocks_ref, *refs):
-    gathered, out_ref = refs[:-1], refs[-1]
+    gathered, mine_ref, other_ref = refs[:-2], refs[-2], refs[-1]
     slots = blocks_ref.shape[3]
-    out_ref[...] = jnp.zeros_like(out_ref)
+    mine_ref[...] = jnp.zeros_like(mine_ref)
+    other_ref[...] = jnp.zeros_like(other_ref)
+    me = lax.axis_index("core")
     targets, source_levels = target_ref[0, 0, tier], level_ref[0, 0, tier]
     positions, count = position_ref[0, 0, tier], count_ref[0, 0][tier]
     products = []
     for s in range(slots):
         position = positions[s]
-        near, far = position % 2, position // 2
-        operand = gathered[0][near, far]
+        operand = gathered[0][position]
         for other in range(1, tier + 1):
-            operand = jnp.where(source_levels[s] == other, gathered[other][near, far], operand)
+            operand = jnp.where(source_levels[s] == other, gathered[other][position], operand)
         operand = jnp.where(s < count, operand, 0.0)
         products.append(product(operand, blocks_ref[0, 0, tier, s]))
     for s in range(slots):
-        target = targets[s]
-        out_ref[target] = out_ref[target] + products[s]
+        chip, is_mine = targets[s] // 2, targets[s] % 2 == me
+        mine_ref[chip] = mine_ref[chip] + jnp.where(is_mine, products[s], 0.0)
+        other_ref[chip] = other_ref[chip] + jnp.where(is_mine, 0.0, products[s])
 
 
 def call(kernel, outs, in_spaces, name, scratch=(), grant=16 << 20):
@@ -158,9 +160,15 @@
     )
 
 
-def collect(copies):
-    strided = lax.all_to_all(copies, "far", 0, 0, tiled=True)
-    return lax.all_gather(strided, "near", axis=0, tiled=False)
+def add_kernel(mine_ref, traded_ref, sum_ref):
+    sum_ref[...] = mine_ref[...] + traded_ref[1 - lax.axis_index("core")]
+
+
+def sum_at_owner(mine, other):
+    traded = lax.all_gather(other, "core", axis=0, tiled=False)
+    shape = jax.ShapeDtypeStruct(mine.shape, mine.dtype)
+    both = call(add_kernel, shape, (VMEM, VMEM), "add")(mine, traded)
+    return lax.all_to_all(both, "chip", 0, 0, tiled=True)
 
 
 def per_device(
@@ -169,11 +177,10 @@
     level_total = right_side.shape[0]
     block = right_side.shape[3:]
     width = block[1]
-    row_peers = lax.axis_size("chip") * lax.axis_size("core")
     f32 = jnp.float32
     solved_shape = jax.ShapeDtypeStruct(block, f32)
-    copies_shape = jax.ShapeDtypeStruct((lax.axis_size("far"), *block), f32)
-    partial_shape = jax.ShapeDtypeStruct((row_peers, *block), f32)
+    copies_shape = jax.ShapeDtypeStruct((lax.axis_size("col"), *block), f32)
+    partial_shape = jax.ShapeDtypeStruct((lax.axis_size("chip"), *block), f32)
     out_shape = jax.ShapeDtypeStruct((level_total, *block), f32)
     inverse_shape = jax.ShapeDtypeStruct((level_total - 1, width, width), f32)
 
@@ -190,14 +197,14 @@
     right_side, off_blocks, *slot_tables = kept
     results, gathered = [solved], []
     for level in range(1, level_total):
-        gathered.append(collect(copies))
-        partial = call(
+        gathered.append(lax.all_to_all(copies, "col", 0, 0, tiled=True))
+        mine, other = call(
             functools.partial(product_kernel, level - 1),
-            partial_shape,
+            (partial_shape, partial_shape),
             (VMEM,) * (level + 5),
             "products",
         )(*slot_tables, off_blocks, *gathered)
-        received = lax.all_to_all(partial, ("chip", "core"), 0, 0, tiled=True)
+        received = sum_at_owner(mine, other)
         if level + 1 < level_total:
             solved, copies = call(
                 functools.partial(solve_kernel, level),
@@ -215,10 +222,8 @@
 
 def solution(mesh):
     rows, cols = mesh.shape["row"], mesh.shape["col"]
-    fine = Mesh(
-        mesh.devices.reshape(rows // 2, 2, cols // 2, 2), ("chip", "core", "far", "near")
-    )
-    row, col = ("chip", "core"), ("far", "near")
+    fine = Mesh(mesh.devices.reshape(rows // 2, 2, cols), ("chip", "core", "col"))
+    row, col = ("chip", "core"), "col"
     placed = (
         P(None, row, col, None, None),
         P(None, row, col, None, None),

time: 184 us -> 173 us (0.940)
  blocking collectives: 176 us -> 164 us
    all_to_all x8, blocking collectives: 155 us -> 130 us  [the longest x4 82.7 us: per_device(): gathered.append(lax.all_to_all(copies, 'col', 0, 0, tiled=True))]
    all_gather x4, blocking collectives: 20.3 us -> 33.6 us  [sum_at_owner(): traded = lax.all_gather(other, 'core', axis=0, tiled=False)]
where the time goes in v3:
time: 173 us; the launch traced here: 172 us
  blocking collectives  164 us (95%)
  Pallas kernels  8.5 us (5%)
    all_to_all x4, blocking collectives, per_device(): gathered.append(lax.all_to_all(copies, 'col', 0, 0, tiled=True))  82.7 us
    all_to_all x4, blocking collectives, sum_at_owner(): return lax.all_to_all(both, 'chip', 0, 0, tiled=True)  47.3 us
    all_gather x4, blocking collectives, sum_at_owner(): traded = lax.all_gather(other, 'core', axis=0, tiled=False)  33.6 us
    pallas_call x1, Pallas kernels, per_device(): call(first_kernel, (inverse_shape, solved_shape, copies_shape, *kept_shap...  4.81 us

profile of v3, /device:TPU:1, one launch (start us, length us, event | category | flops | bytes accessed | tf_op | source)
XLA Modules:
  0.0 172.2 jit_solution(6708546794493190342)
XLA Ops:
  0.0 4.8 %first.1 = (f32[4,128,128]{2,1,0:T(8,128)S(1)}, f32[32,128]{1,0:T(8,128)S(1)}, f32[16,32,128]{2,1,0:T(8,128)S(1)}, f32[5,1,1,32,128]{4,3,2,1,0:T(8,128)S(1)}, f3...) custom-call(f32[5,1,1,128,128]{4,3,2,1,0:T(8,128)} %refs_0_.1, ...), custom_call_target="tpu_custom_call" | custom-call | flops 67108864 | bytes 1048576 | tf_op jit(solution)/shard_map/first/pallas_call | solution.py:189
  4.8 29.3 %all_to_all.40.refs_0_ = f32[16,32,128]{2,1,0:T(8,128)S(1)} all-to-all(f32[16,32,128]{2,1,0:T(8,128)S(1)} %get-tuple-element.33), channel_id=1, replica_groups=mesh['chip'=16,'core'=2,'col'=16] {'col'}, dimensions={0} | all-to-all | bytes 524288 | tf_op jit(solution)/shard_map/all_to_all | solution.py:200
  34.1 0.5 products.4
  34.6 7.4 %all-gather = f32[32,32,128]{2,1,0:T(8,128)S(1)} all-gather(f32[16,32,128]{2,1,0:T(8,128)S(1)} %get-tuple-element.35), channel_id=2, replica_groups=mesh['chip'=16,'core'=2,'col'=16] {'core'}, dimensions={0}, use_global_device_ids=true | all-gather | bytes 786432 | tf_op jit(solution)/shard_map/all_gather | solution.py:168
  42.0 14.1 %all_to_all.41.received_ref = f32[16,32,128]{2,1,0:T(8,128)S(1)} all-to-all(f32[16,32,128]{2,1,0:T(8,128)S(1)} %add.4), channel_id=1, replica_groups=mesh['chip'=16,'core'=2,'col'=16] {'chip'}, dimensions={0} | all-to-all | bytes 524288 | tf_op jit(solution)/shard_map/all_to_all | solution.py:171
  56.1 0.2 solve.3
  56.4 18.0 %all_to_all.42.refs_1_ = f32[16,32,128]{2,1,0:T(8,128)S(1)} all-to-all(f32[16,32,128]{2,1,0:T(8,128)S(1)} %get-tuple-element.38), channel_id=1, replica_groups=mesh['chip'=16,'core'=2,'col'=16] {'col'}, dimensions={0} | all-to-all | bytes 524288 | tf_op jit(solution)/shard_map/all_to_all | solution.py:200
  74.4 0.5 products.5
  74.9 8.7 %all-gather.1 = f32[32,32,128]{2,1,0:T(8,128)S(1)} all-gather(f32[16,32,128]{2,1,0:T(8,128)S(1)} %get-tuple-element.40), channel_id=3, replica_groups=mesh['chip'=16,'core'=2,'col'=16] {'core'}, dimensions={0}, use_global_device_ids=true | all-gather | bytes 786432 | tf_op jit(solution)/shard_map/all_gather | solution.py:168
  83.7 11.1 %all_to_all.43.received_ref = f32[16,32,128]{2,1,0:T(8,128)S(1)} all-to-all(f32[16,32,128]{2,1,0:T(8,128)S(1)} %add.5), channel_id=1, replica_groups=mesh['chip'=16,'core'=2,'col'=16] {'chip'}, dimensions={0} | all-to-all | bytes 524288 | tf_op jit(solution)/shard_map/all_to_all | solution.py:171
  94.7 0.2 solve.4
  95.0 17.7 %all_to_all.44.refs_2_ = f32[16,32,128]{2,1,0:T(8,128)S(1)} all-to-all(f32[16,32,128]{2,1,0:T(8,128)S(1)} %get-tuple-element.41), channel_id=1, replica_groups=mesh['chip'=16,'core'=2,'col'=16] {'col'}, dimensions={0} | all-to-all | bytes 524288 | tf_op jit(solution)/shard_map/all_to_all | solution.py:200
  112.7 0.5 products.6
  113.2 8.7 %all-gather.2 = f32[32,32,128]{2,1,0:T(8,128)S(1)} all-gather(f32[16,32,128]{2,1,0:T(8,128)S(1)} %get-tuple-element.43), channel_id=4, replica_groups=mesh['chip'=16,'core'=2,'col'=16] {'core'}, dimensions={0}, use_global_device_ids=true | all-gather | bytes 786432 | tf_op jit(solution)/shard_map/all_gather | solution.py:168
  122.0 11.1 %all_to_all.45.received_ref = f32[16,32,128]{2,1,0:T(8,128)S(1)} all-to-all(f32[16,32,128]{2,1,0:T(8,128)S(1)} %add.6), channel_id=1, replica_groups=mesh['chip'=16,'core'=2,'col'=16] {'chip'}, dimensions={0} | all-to-all | bytes 524288 | tf_op jit(solution)/shard_map/all_to_all | solution.py:171
  133.1 0.2 solve.5
  133.3 17.7 %all_to_all.46.refs_3_ = f32[16,32,128]{2,1,0:T(8,128)S(1)} all-to-all(f32[16,32,128]{2,1,0:T(8,128)S(1)} %get-tuple-element.44), channel_id=1, replica_groups=mesh['chip'=16,'core'=2,'col'=16] {'col'}, dimensions={0} | all-to-all | bytes 524288 | tf_op jit(solution)/shard_map/all_to_all | solution.py:200
  151.0 0.5 products.7
  151.5 8.7 %all-gather.3 = f32[32,32,128]{2,1,0:T(8,128)S(1)} all-gather(f32[16,32,128]{2,1,0:T(8,128)S(1)} %get-tuple-element.46), channel_id=5, replica_groups=mesh['chip'=16,'core'=2,'col'=16] {'core'}, dimensions={0}, use_global_device_ids=true | all-gather | bytes 786432 | tf_op jit(solution)/shard_map/all_gather | solution.py:168
  160.3 11.1 %all_to_all.47.received_ref = f32[16,32,128]{2,1,0:T(8,128)S(1)} all-to-all(f32[16,32,128]{2,1,0:T(8,128)S(1)} %add.7), channel_id=1, replica_groups=mesh['chip'=16,'core'=2,'col'=16] {'chip'}, dimensions={0} | all-to-all | bytes 524288 | tf_op jit(solution)/shard_map/all_to_all | solution.py:171
  171.4 0.9 last.1
  (4 shorter events, 0.1 us)

commit v4 on v2

v4 whole, which is shorter than its diff:
```python
import functools

import jax
import jax.numpy as jnp
from jax import lax
from jax.experimental import pallas as pl
from jax.experimental.pallas import tpu as pltpu
from jax.sharding import Mesh
from jax.sharding import PartitionSpec as P

HIGHEST = lax.Precision.HIGHEST
VMEM = pltpu.VMEM
BASE = 32
GRANT = 16 << 20


def mm(a, b):
    return jnp.dot(a, b, precision=HIGHEST, preferred_element_type=jnp.float32)


def mm_nt(a, b):
    return lax.dot_general(
        a, b, (((1,), (1,)), ((), ())), precision=HIGHEST, preferred_element_type=jnp.float32
    )


def invert_lower(blocks):
    size = blocks[0].shape[0]
    rows = lax.broadcasted_iota(jnp.int32, (size, size), 0)
    cols = lax.broadcasted_iota(jnp.int32, (size, size), 1)
    eye = rows == cols
    strict = rows > cols
    same = (rows // BASE) == (cols // BASE)
    scaled, scale_cols, powers, inverses = [], [], [], []
    for block in blocks:
        on_diag = jnp.where(eye, block, 0.0)
        scale_rows = 1.0 / jnp.sum(on_diag, axis=1, keepdims=True)
        scale_cols.append(1.0 / jnp.sum(on_diag, axis=0, keepdims=True))
        m = jnp.where(strict, block * scale_rows, 0.0)
        scaled.append(m)
        local = jnp.where(same, m, 0.0)
        powers.append(local)
        inverses.append(jnp.where(eye, 1.0, 0.0) - local)
    span = 2
    while span < BASE:
        powers = [mm(p, p) for p in powers]
        inverses = [v + mm(v, p) for v, p in zip(inverses, powers)]
        span *= 2
    width = BASE
    while width < size:
        joins = ((rows // (2 * width)) == (cols // (2 * width))) & (
            (rows // width) > (cols // width)
        )
        steps = [mm(jnp.where(joins, m, 0.0), v) for m, v in zip(scaled, inverses)]
        inverses = [v - mm(v, s) for v, s in zip(inverses, steps)]
        width *= 2
    return [v * s for v, s in zip(inverses, scale_cols)]


def first_kernel(*refs):
    diag_hbm, right_hbm, blocks_hbm = refs[:3]
    tables_hbm = refs[3:7]
    packed_ref, solved_ref, blocks_ref = refs[7:10]
    diag_ref, right_ref = refs[10:12]
    table_refs, sems = refs[12:16], refs[16]
    sources = (diag_hbm, right_hbm, *tables_hbm, blocks_hbm)
    targets = (diag_ref, right_ref, *table_refs, blocks_ref)
    moves = [
        pltpu.make_async_copy(source, target, sems.at[at])
        for at, (source, target) in enumerate(zip(sources, targets))
    ]
    for move in moves:
        move.start()
    moves[0].wait()
    moves[1].wait()
    level_total, width = diag_ref.shape[0], diag_ref.shape[-1]
    inverses = invert_lower([diag_ref[level, 0, 0] for level in range(level_total)])
    solved = mm_nt(right_ref[0, 0, 0], inverses[0])
    solved_ref[...] = solved
    at = Layout(level_total, *right_ref.shape[3:], table_refs[0].shape[2])
    packed_ref[at.solved : at.right] = solved
    for tier in range(level_total - 1):
        packed_ref[tier * width : (tier + 1) * width] = inverses[tier + 1]
        begin = at.right + tier * at.width_rhs
        packed_ref[begin : begin + at.width_rhs] = right_ref[tier + 1, 0, 0]
    packed_ref[at.tables : at.rows] = jnp.zeros((at.rows - at.tables, width), jnp.float32)
    for move in moves[2:-1]:
        move.wait()
    for table, ref in enumerate(table_refs[:3]):
        begin = at.tables + table * at.tiers
        packed_ref[begin : begin + at.tiers, : ref.shape[3]] = ref[0, 0].astype(jnp.float32)
    begin = at.tables + 3 * at.tiers
    packed_ref[begin : begin + 1, : at.tiers] = table_refs[3][0].astype(jnp.float32)
    moves[-1].wait()


class Layout:
    def __init__(self, level_total, width_rhs, width, tiers):
        self.width_rhs, self.width, self.tiers = width_rhs, width, tiers
        self.solved = (level_total - 1) * width
        self.right = self.solved + width_rhs
        self.tables = self.right + (level_total - 1) * width_rhs
        self.rows = self.tables + 4 * tiers

    def half(self, begin, me):
        size = self.width_rhs // 2
        return pl.ds(pl.multiple_of(begin + me * size, size), size)


def copy_to_all(copies_ref, row, value):
    for peer in range(copies_ref.shape[0]):
        copies_ref[peer, row] = value


def spread_kernel(at, both_ref, copies_ref):
    me = lax.axis_index("core")
    for row in range(2):
        copy_to_all(copies_ref, row, both_ref[row, at.half(at.solved, me)])


def reduced_solve(at, level, received_ref, both_ref):
    me = lax.axis_index("core")
    total = received_ref[0]
    for peer in range(1, received_ref.shape[0]):
        total = total + received_ref[peer]
    begin = at.right + (level - 1) * at.width_rhs
    inverse = pl.ds((level - 1) * at.width, at.width)
    return [
        mm_nt(both_ref[row, at.half(begin, me)] - total[row], both_ref[row, inverse])
        for row in range(2)
    ]


def solve_kernel(at, level, received_ref, both_ref, solved_ref, copies_ref):
    for row, solved in enumerate(reduced_solve(at, level, received_ref, both_ref)):
        solved_ref[row] = solved
        copy_to_all(copies_ref, row, solved)


def last_kernel(at, received_ref, both_ref, *refs):
    earlier, (mine_ref, other_ref, last_ref) = refs[:-3], refs[-3:]
    me = lax.axis_index("core")
    level = len(earlier) + 1
    for row, solved in enumerate(reduced_solve(at, level, received_ref, both_ref)):
        last_ref[row] = solved
    for tier, ref in enumerate((*earlier, last_ref)):
        mine_ref[tier] = ref[me]
        other_ref[tier] = ref[1 - me]


def join_kernel(solved_ref, mine_ref, traded_ref, out_ref):
    me = lax.axis_index("core")
    size = mine_ref.shape[1]
    out_ref[0] = solved_ref[...]
    for tier in range(mine_ref.shape[0]):
        out_ref[tier + 1, pl.ds(pl.multiple_of(me * size, size), size)] = mine_ref[tier]
        out_ref[tier + 1, pl.ds(pl.multiple_of((1 - me) * size, size), size)] = traded_ref[
            1 - me, tier
        ]


def split(value):
    high = value.astype(jnp.bfloat16)
    return high, (value - high.astype(jnp.float32)).astype(jnp.bfloat16)


def product(operand, block):
    rows = operand.shape[0]
    operand_high, operand_low = split(operand)
    block_high, block_low = split(block)
    contract = (((1,), (1,)), ((), ()))
    both = lax.dot_general(
        jnp.concatenate([operand_high, operand_low], axis=0),
        block_high,
        contract,
        preferred_element_type=jnp.float32,
    )
    rest = lax.dot_general(
        operand_high, block_low, contract, preferred_element_type=jnp.float32
    )
    return both[:rows] + (both[rows:] + rest)


def product_kernel(at, tier, both_ref, own_ref, other_ref, *refs):
    gathered, out_ref = refs[:-1], refs[-1]
    slots = own_ref.shape[3]
    out_ref[...] = jnp.zeros_like(out_ref)
    me = lax.axis_index("core")
    found = []
    for row, blocks_ref in ((me, own_ref), (1 - me, other_ref)):
        tables = [both_ref[row, at.tables + table * at.tiers + tier] for table in range(3)]
        targets, source_levels, positions = (table.astype(jnp.int32) for table in tables)
        counts = both_ref[row, at.tables + 3 * at.tiers].astype(jnp.int32)
        for s in range(slots):
            position = positions[s]
            operand = gathered[0][position, row]
            for other in range(1, tier + 1):
                operand = jnp.where(
                    source_levels[s] == other, gathered[other][position, row], operand
                )
            operand = jnp.where(s < counts[tier], operand, 0.0)
            found.append((targets[s], product(operand, blocks_ref[0, 0, tier, s])))
    for target, value in found:
        out_ref[target // 2, target % 2] = out_ref[target // 2, target % 2] + value


def call(kernel, outs, in_spaces, name, scratch=(), grant=16 << 20):
    return pl.pallas_call(
        kernel,
        out_shape=outs,
        in_specs=[pl.BlockSpec(memory_space=space) for space in in_spaces],
        out_specs=jax.tree.map(lambda _: pl.BlockSpec(memory_space=VMEM), outs),
        cost_estimate=pl.CostEstimate(flops=1 << 26, bytes_accessed=1 << 20, transcendentals=0),
        scratch_shapes=scratch,
        compiler_params=pltpu.CompilerParams(vmem_limit_bytes=grant),
        name=name,
    )


def per_device(
    right_side, diag_blocks, off_blocks, slot_target, slot_level, slot_position, slot_count
):
    level_total, _, _, width_rhs, width = right_side.shape
    tiers = level_total - 1
    at = Layout(level_total, width_rhs, width, tiers)
    half = (width_rhs // 2, width)

    def shape(*dims):
        return jax.ShapeDtypeStruct(dims, jnp.float32)

    solved_shape = shape(2, *half)
    copies_shape = shape(lax.axis_size("col"), 2, *half)
    partial_shape = shape(lax.axis_size("chip"), 2, *half)
    part_shape = shape(tiers, *half)
    inputs = (
        diag_blocks, right_side, off_blocks, slot_target, slot_level, slot_position, slot_count
    )

    packed, first_solved, own_blocks = call(
        first_kernel,
        (shape(at.rows, width), shape(width_rhs, width), shape(*off_blocks.shape)),
        (pltpu.HBM,) * 7,
        "first",
        (
            *(pltpu.VMEM(x.shape, x.dtype) for x in inputs[:2] + inputs[3:]),
            pltpu.SemaphoreType.DMA((7,)),
        ),
    )(*(pltpu.with_memory_space_constraint(x, pltpu.HBM) for x in inputs))
    other_blocks = lax.ppermute(off_blocks, "core", [(0, 1), (1, 0)])
    both = lax.all_gather(packed, "core", axis=0, tiled=False)
    copies = call(functools.partial(spread_kernel, at), copies_shape, (VMEM,), "spread")(both)
    results, gathered = [], []
    for level in range(1, level_total):
        gathered.append(lax.all_to_all(copies, "col", 0, 0, tiled=True))
        partial = call(
            functools.partial(product_kernel, at, level - 1),
            partial_shape,
            (VMEM,) * (3 + level),
            "products",
        )(both, own_blocks, other_blocks, *gathered)
        received = lax.all_to_all(partial, "chip", 0, 0, tiled=True)
        if level + 1 < level_total:
            solved, copies = call(
                functools.partial(solve_kernel, at, level),
                (solved_shape, copies_shape),
                (VMEM,) * 2,
                "solve",
            )(received, both)
            results.append(solved)
    mine, other, _ = call(
        functools.partial(last_kernel, at),
        (part_shape, part_shape, solved_shape),
        (VMEM,) * (2 + len(results)),
        "last",
    )(received, both, *results)
    traded = lax.all_gather(other, "core", axis=0, tiled=False)
    out = call(join_kernel, shape(level_total, width_rhs, width), (VMEM,) * 3, "join")(
        first_solved, mine, traded
    )
    return out[:, None, None]


def solution(mesh):
    rows, cols = mesh.shape["row"], mesh.shape["col"]
    fine = Mesh(mesh.devices.reshape(rows // 2, 2, cols), ("chip", "core", "col"))
    row, col = ("chip", "core"), "col"
    placed = (
        P(None, row, col, None, None),
        P(None, row, col, None, None),
        P(row, col, None, None, None, None),
        P(row, col, None, None),
        P(row, col, None, None),
        P(row, col, None, None),
        P(row, col, None),
    )
    return jax.shard_map(
        per_device,
        mesh=fine,
        in_specs=placed,
        out_specs=P(None, row, col, None, None),
        check_vma=False,
    )
```

time: 184 us -> 170 us (0.924)
  blocking collectives: 176 us -> 150 us
  starting transfers between devices: 0 us -> 8.73 us
  Pallas kernels: 8.31 us -> 10.3 us
    all_to_all x8, blocking collectives: 155 us -> 138 us  [the longest x4 91.4 us: per_device(): gathered.append(lax.all_to_all(copies, 'col', 0, 0, tiled=True))]
    ppermute x0 -> x1, starting transfers between devices: none -> 8.73 us  [per_device(): other_blocks = lax.ppermute(off_blocks, 'core', [(0, 1), (1, 0)])]
    all_gather x4 -> x2, blocking collectives: 20.3 us -> 12.6 us  [the longest x1 10.2 us: per_device(): traded = lax.all_gather(other, 'core', axis=0, tiled=False)]
    pallas_call x9 -> x11, Pallas kernels: 8.31 us -> 10.3 us  [the longest x1 4.79 us: per_device(): call(first_kernel, (shape(at.rows, width), shape(width_rhs, width), shape...]
  transfers between devices with their start and end apart: 0 -> 1, of which waited for: 0 -> 0; matrix products, arithmetic and copies ran while one was open for 0% -> 0% of each run, Pallas kernels for 0% -> 3%
where the time goes in v4:
time: 170 us; the launch traced here: 169 us
  blocking collectives  150 us (88%)
  Pallas kernels  10.3 us (6%)
  starting transfers between devices  8.73 us (5%)
    all_to_all x4, blocking collectives, per_device(): gathered.append(lax.all_to_all(copies, 'col', 0, 0, tiled=True))  91.4 us
    all_to_all x4, blocking collectives, per_device(): received = lax.all_to_all(partial, 'chip', 0, 0, tiled=True)  46.1 us
    all_gather x1, blocking collectives, per_device(): traded = lax.all_gather(other, 'core', axis=0, tiled=False)  10.2 us
    ppermute x1, starting transfers between devices, per_device(): other_blocks = lax.ppermute(off_blocks, 'core', [(0, 1), (1, 0)])  8.73 us
    pallas_call x1, Pallas kernels, per_device(): call(first_kernel, (shape(at.rows, width), shape(width_rhs, width), shape...  4.79 us
  transfers between devices with their start and end apart: 1, of which 0 were waited for; matrix products, arithmetic and copies ran while one was open for 0% of the time, Pallas kernels for 3%

profile of v4, /device:TPU:1, one launch (start us, length us, event | category | flops | bytes accessed | tf_op | source)
XLA Modules:
  0.0 169.2 jit_solution(17131977540391356211)
XLA Ops:
  0.0 8.7 %collective-permute-start = (f32[1,1,4,8,128,128]{5,4,3,2,1,0:T(8,128)}, f32[1,1,4,8,128,128]{5,4,3,2,1,0:T(8,128)S(1)}, u32[]{:S(2)}, u32[]{:S(2)}) collective-permute-start(f32[1,1,4,8,128,128]{5,4,3,2,1,0:T(8,128)} %refs_2_.1), channel_id=1, source_target_pairs={{0,16},{16,0},{1,17},{17,1},{2,18},{18,2},{3,19},{19,3},{4,20},{20... | collective-permute-start | bytes 6291464 | tf_op jit(solution)/shard_map/ppermute | solution.py:249
  8.7 4.8 %first.1 = (f32[688,128]{1,0:T(8,128)S(1)}, f32[32,128]{1,0:T(8,128)S(1)}, f32[1,1,4,8,128,128]{5,4,3,2,1,0:T(8,128)S(1)}) custom-call(f32[5,1,1,128,128]{4,3,2,1,0:T(8,128)} %refs_0_.1, f32[5,1,1,32,128]{4,3,2,1,0:T(8,128)} %refs_1_.1, f32[1,1,4,8,128,128]{5,4,3,2,1,0:T(8,128)} %refs_2_.1, s32[1,1,4,8]{3,2,1,0:T(4,128)} %refs_3_.1, s32[1,1,4,8]{3,2,1,0:T(4,128)} %refs_4_.1, ...), custom_call_target="tpu_custom_call" | custom-call | flops 67108864 | bytes 1048576 | tf_op jit(solution)/shard_map/first/pallas_call | solution.py:239
  13.5 2.3 %all-gather = f32[1376,128]{1,0:T(8,128)S(1)} all-gather(f32[688,128]{1,0:T(8,128)S(1)} %get-tuple-element.17), channel_id=2, replica_groups=mesh['chip'=16,'core'=2,'col'=16] {'core'}, dimensions={0}, use_global_device_ids=true | all-gather | bytes 1056768 | tf_op jit(solution)/shard_map/all_gather | solution.py:250
  15.9 23.5 %all_to_all.40.refs_0_ = f32[16,2,16,128]{3,2,1,0:T(8,128)S(1)} all-to-all(f32[16,2,16,128]{3,2,1,0:T(8,128)S(1)} %spread.1), channel_id=1, replica_groups=mesh['chip'=16,'core'=2,'col'=16] {'col'}, dimensions={0} | all-to-all | bytes 524288 | tf_op jit(solution)/shard_map/all_to_all | solution.py:254
  39.4 0.0 collective-permute-done.other_ref
  39.4 0.7 products.4
  40.1 13.9 %all_to_all.41.received_ref = f32[16,2,16,128]{3,2,1,0:T(8,128)S(1)} all-to-all(f32[16,2,16,128]{3,2,1,0:T(8,128)S(1)} %products.4), channel_id=1, replica_groups=mesh['chip'=16,'core'=2,'col'=16] {'chip'}, dimensions={0} | all-to-all | bytes 524288 | tf_op jit(solution)/shard_map/all_to_all | solution.py:261
  54.0 0.3 solve.3
  54.4 22.7 %all_to_all.42.refs_1_ = f32[16,2,16,128]{3,2,1,0:T(8,128)S(1)} all-to-all(f32[16,2,16,128]{3,2,1,0:T(8,128)S(1)} %get-tuple-element.19), channel_id=1, replica_groups=mesh['chip'=16,'core'=2,'col'=16] {'col'}, dimensions={0} | all-to-all | bytes 524288 | tf_op jit(solution)/shard_map/all_to_all | solution.py:254
  77.1 0.7 products.5
  77.8 10.8 %all_to_all.43.received_ref = f32[16,2,16,128]{3,2,1,0:T(8,128)S(1)} all-to-all(f32[16,2,16,128]{3,2,1,0:T(8,128)S(1)} %products.5), channel_id=1, replica_groups=mesh['chip'=16,'core'=2,'col'=16] {'chip'}, dimensions={0} | all-to-all | bytes 524288 | tf_op jit(solution)/shard_map/all_to_all | solution.py:261
  88.6 0.3 solve.4
  89.0 22.9 %all_to_all.44.refs_2_ = f32[16,2,16,128]{3,2,1,0:T(8,128)S(1)} all-to-all(f32[16,2,16,128]{3,2,1,0:T(8,128)S(1)} %get-tuple-element.20), channel_id=1, replica_groups=mesh['chip'=16,'core'=2,'col'=16] {'col'}, dimensions={0} | all-to-all | bytes 524288 | tf_op jit(solution)/shard_map/all_to_all | solution.py:254
  111.8 0.7 products.6
  112.6 10.8 %all_to_all.45.received_ref = f32[16,2,16,128]{3,2,1,0:T(8,128)S(1)} all-to-all(f32[16,2,16,128]{3,2,1,0:T(8,128)S(1)} %products.6), channel_id=1, replica_groups=mesh['chip'=16,'core'=2,'col'=16] {'chip'}, dimensions={0} | all-to-all | bytes 524288 | tf_op jit(solution)/shard_map/all_to_all | solution.py:261
  123.3 0.3 solve.5
  123.7 22.2 %all_to_all.46.refs_3_ = f32[16,2,16,128]{3,2,1,0:T(8,128)S(1)} all-to-all(f32[16,2,16,128]{3,2,1,0:T(8,128)S(1)} %get-tuple-element.21), channel_id=1, replica_groups=mesh['chip'=16,'core'=2,'col'=16] {'col'}, dimensions={0} | all-to-all | bytes 524288 | tf_op jit(solution)/shard_map/all_to_all | solution.py:254
  145.9 0.8 products.7
  146.6 10.7 %all_to_all.47.received_ref = f32[16,2,16,128]{3,2,1,0:T(8,128)S(1)} all-to-all(f32[16,2,16,128]{3,2,1,0:T(8,128)S(1)} %products.7), channel_id=1, replica_groups=mesh['chip'=16,'core'=2,'col'=16] {'chip'}, dimensions={0} | all-to-all | bytes 524288 | tf_op jit(solution)/shard_map/all_to_all | solution.py:261
  157.4 0.9 last.1
  158.3 10.2 %all-gather.1 = f32[8,16,128]{2,1,0:T(8,128)S(1)} all-gather(f32[4,16,128]{2,1,0:T(8,128)S(1)} %get-tuple-element.26), channel_id=3, replica_groups=mesh['chip'=16,'core'=2,'col'=16] {'core'}, dimensions={0}, use_global_device_ids=true | all-gather | bytes 98304 | tf_op jit(solution)/shard_map/all_gather | solution.py:276
  168.5 0.6 join.1
  (1 shorter events, 0.0 us)
Async XLA Ops:
  0.0 39.4 %collective-permute-start = (f32[1,1,4,8,128,128]{5,4,3,2,1,0:T(8,128)}, f32[1,1,4,8,128,128]{5,4,3,2,1,0:T(8,128)S(1)}, u32[]{:S(2)}, u32[]{:S(2)}) collective-permute-start(f32[1,1,4,8,128,128]{5,4,3,2,1,0:T(8,128)} %refs_2_.1), channel_id=1, source_target_pairs={{0,16},{16,0},{1,17},{17,1},{2,18},{18,2},{3,19},{19,3},{4,20},{20... | collective-permute-start | bytes 6291464 | tf_op jit(solution)/shard_map/ppermute | solution.py:249

commit v5 on v4

--- a/solution.py
+++ b/solution.py
@@ -12,6 +12,7 @@
 VMEM = pltpu.VMEM
 BASE = 32
 GRANT = 16 << 20
+HEAD_START = 2500
 
 
 def mm(a, b):
@@ -112,8 +113,10 @@
         copies_ref[peer, row] = value
 
 
-def spread_kernel(at, both_ref, copies_ref):
-    me = lax.axis_index("core")
+def spread_kernel(at, both_ref, copies_ref, spent_ref):
+    me = lax.axis_index("core")
+    steps = jnp.where(me == 1, HEAD_START, 0)
+    spent_ref[0] = lax.fori_loop(0, steps, lambda i, v: v * 5 + i, me)
     for row in range(2):
         copy_to_all(copies_ref, row, both_ref[row, at.half(at.solved, me)])
 
@@ -204,7 +207,7 @@
         out_ref[target // 2, target % 2] = out_ref[target // 2, target % 2] + value
 
 
-def call(kernel, outs, in_spaces, name, scratch=(), grant=16 << 20):
+def call(kernel, outs, in_spaces, name, scratch=()):
     return pl.pallas_call(
         kernel,
         out_shape=outs,
@@ -212,7 +215,7 @@
         out_specs=jax.tree.map(lambda _: pl.BlockSpec(memory_space=VMEM), outs),
         cost_estimate=pl.CostEstimate(flops=1 << 26, bytes_accessed=1 << 20, transcendentals=0),
         scratch_shapes=scratch,
-        compiler_params=pltpu.CompilerParams(vmem_limit_bytes=grant),
+        compiler_params=pltpu.CompilerParams(vmem_limit_bytes=GRANT),
         name=name,
     )
 
@@ -248,7 +251,13 @@
     )(*(pltpu.with_memory_space_constraint(x, pltpu.HBM) for x in inputs))
     other_blocks = lax.ppermute(off_blocks, "core", [(0, 1), (1, 0)])
     both = lax.all_gather(packed, "core", axis=0, tiled=False)
-    copies = call(functools.partial(spread_kernel, at), copies_shape, (VMEM,), "spread")(both)
+    copies = call(
+        functools.partial(spread_kernel, at),
+        copies_shape,
+        (VMEM,),
+        "spread",
+        (pltpu.SMEM((1,), jnp.int32),),
+    )(both)
     results, gathered = [], []
     for level in range(1, level_total):
         gathered.append(lax.all_to_all(copies, "col", 0, 0, tiled=True))
@@ -267,11 +276,12 @@
                 "solve",
             )(received, both)
             results.append(solved)
-    mine, other, _ = call(
+    mine, other = call(
         functools.partial(last_kernel, at),
-        (part_shape, part_shape, solved_shape),
+        (part_shape, part_shape),
         (VMEM,) * (2 + len(results)),
         "last",
+        (pltpu.VMEM((2, *half), jnp.float32),),
     )(received, both, *results)
     traded = lax.all_gather(other, "core", axis=0, tiled=False)
     out = call(join_kernel, shape(level_total, width_rhs, width), (VMEM,) * 3, "join")(

time: 170 us -> 162 us (0.953)
  blocking collectives: 150 us -> 130 us
  Pallas kernels: 10.3 us -> 22.5 us
    pallas_call x2, Pallas kernels: 0.94 us -> 13.1 us  [the longest x1 12.8 us: per_device(): call(functools.partial(spread_kernel, at), copies_shape, (VMEM,), 'spread...]
    all_to_all x4, blocking collectives: 91.4 us -> 80.2 us  [per_device(): gathered.append(lax.all_to_all(copies, 'col', 0, 0, tiled=True))]
    all_gather x1, blocking collectives: 10.2 us -> 1.86 us  [per_device(): traded = lax.all_gather(other, 'core', axis=0, tiled=False)]
  transfers between devices with their start and end apart: 1 -> 1, of which waited for: 0 -> 0; matrix products, arithmetic and copies ran while one was open for 0% -> 0% of each run, Pallas kernels for 3% -> 11%
where the time goes in v5:
time: 162 us; the launch traced here: 161 us
  blocking collectives  130 us (80%)
  Pallas kernels  22.5 us (14%)
  starting transfers between devices  8.73 us (5%)
    all_to_all x4, blocking collectives, per_device(): gathered.append(lax.all_to_all(copies, 'col', 0, 0, tiled=True))  80.2 us
    all_to_all x4, blocking collectives, per_device(): received = lax.all_to_all(partial, 'chip', 0, 0, tiled=True)  45.7 us
    pallas_call x1, Pallas kernels, per_device(): call(functools.partial(spread_kernel, at), copies_shape, (VMEM,), 'spread...  12.8 us
    ppermute x1, starting transfers between devices, per_device(): other_blocks = lax.ppermute(off_blocks, 'core', [(0, 1), (1, 0)])  8.73 us
    pallas_call x1, Pallas kernels, per_device(): call(first_kernel, (shape(at.rows, width), shape(width_rhs, width), shape...  4.79 us
  transfers between devices with their start and end apart: 1, of which 0 were waited for; matrix products, arithmetic and copies ran while one was open for 0% of the time, Pallas kernels for 11%

profile of v5, /device:TPU:1, one launch (start us, length us, event | category | flops | bytes accessed | tf_op | source)
XLA Modules:
  0.0 161.3 jit_solution(13983925398566434520)
XLA Ops:
  0.0 8.7 %collective-permute-start = (f32[1,1,4,8,128,128]{5,4,3,2,1,0:T(8,128)}, f32[1,1,4,8,128,128]{5,4,3,2,1,0:T(8,128)S(1)}, u32[]{:S(2)}, u32[]{:S(2)}) collective-permute-start(f32[1,1,4,8,128,128]{5,4,3,2,1,0:T(8,128)} %refs_2_.1), channel_id=1, source_target_pairs={{0,16},{16,0},{1,17},{17,1},{2,18},{18,2},{3,19},{19,3},{4,20},{20... | collective-permute-start | bytes 6291464 | tf_op jit(solution)/shard_map/ppermute | solution.py:252
  8.7 4.8 %first.1 = (f32[688,128]{1,0:T(8,128)S(1)}, f32[32,128]{1,0:T(8,128)S(1)}, f32[1,1,4,8,128,128]{5,4,3,2,1,0:T(8,128)S(1)}) custom-call(f32[5,1,1,128,128]{4,3,2,1,0:T(8,128)} %refs_0_.1, f32[5,1,1,32,128]{4,3,2,1,0:T(8,128)} %refs_1_.1, f32[1,1,4,8,128,128]{5,4,3,2,1,0:T(8,128)} %refs_2_.1, s32[1,1,4,8]{3,2,1,0:T(4,128)} %refs_3_.1, s32[1,1,4,8]{3,2,1,0:T(4,128)} %refs_4_.1, ...), custom_call_target="tpu_custom_call" | custom-call | flops 67108864 | bytes 1048576 | tf_op jit(solution)/shard_map/first/pallas_call | solution.py:242
  13.5 2.3 %all-gather = f32[1376,128]{1,0:T(8,128)S(1)} all-gather(f32[688,128]{1,0:T(8,128)S(1)} %get-tuple-element.17), channel_id=2, replica_groups=mesh['chip'=16,'core'=2,'col'=16] {'core'}, dimensions={0}, use_global_device_ids=true | all-gather | bytes 1056768 | tf_op jit(solution)/shard_map/all_gather | solution.py:253
  15.9 12.8 %spread.1 = f32[16,2,16,128]{3,2,1,0:T(8,128)S(1)} custom-call(f32[2,688,128]{2,1,0:T(8,128)S(1)} %bitcast.5), custom_call_target="tpu_custom_call" | custom-call | flops 67108864 | bytes 1048576 | tf_op jit(solution)/shard_map/spread/pallas_call | solution.py:254
  28.6 22.1 %all_to_all.40.refs_0_ = f32[16,2,16,128]{3,2,1,0:T(8,128)S(1)} all-to-all(f32[16,2,16,128]{3,2,1,0:T(8,128)S(1)} %spread.1), channel_id=1, replica_groups=mesh['chip'=16,'core'=2,'col'=16] {'col'}, dimensions={0} | all-to-all | bytes 524288 | tf_op jit(solution)/shard_map/all_to_all | solution.py:263
  50.7 0.0 collective-permute-done.other_ref
  50.7 0.7 products.4
  51.4 13.9 %all_to_all.41.received_ref = f32[16,2,16,128]{3,2,1,0:T(8,128)S(1)} all-to-all(f32[16,2,16,128]{3,2,1,0:T(8,128)S(1)} %products.4), channel_id=1, replica_groups=mesh['chip'=16,'core'=2,'col'=16] {'chip'}, dimensions={0} | all-to-all | bytes 524288 | tf_op jit(solution)/shard_map/all_to_all | solution.py:270
  65.3 0.3 solve.3
  65.7 18.6 %all_to_all.42.refs_1_ = f32[16,2,16,128]{3,2,1,0:T(8,128)S(1)} all-to-all(f32[16,2,16,128]{3,2,1,0:T(8,128)S(1)} %get-tuple-element.19), channel_id=1, replica_groups=mesh['chip'=16,'core'=2,'col'=16] {'col'}, dimensions={0} | all-to-all | bytes 524288 | tf_op jit(solution)/shard_map/all_to_all | solution.py:263
  84.3 0.7 products.5
  85.0 10.8 %all_to_all.43.received_ref = f32[16,2,16,128]{3,2,1,0:T(8,128)S(1)} all-to-all(f32[16,2,16,128]{3,2,1,0:T(8,128)S(1)} %products.5), channel_id=1, replica_groups=mesh['chip'=16,'core'=2,'col'=16] {'chip'}, dimensions={0} | all-to-all | bytes 524288 | tf_op jit(solution)/shard_map/all_to_all | solution.py:270
  95.8 0.3 solve.4
  96.2 18.6 %all_to_all.44.refs_2_ = f32[16,2,16,128]{3,2,1,0:T(8,128)S(1)} all-to-all(f32[16,2,16,128]{3,2,1,0:T(8,128)S(1)} %get-tuple-element.20), channel_id=1, replica_groups=mesh['chip'=16,'core'=2,'col'=16] {'col'}, dimensions={0} | all-to-all | bytes 524288 | tf_op jit(solution)/shard_map/all_to_all | solution.py:263
  114.8 0.7 products.6
  115.5 10.5 %all_to_all.45.received_ref = f32[16,2,16,128]{3,2,1,0:T(8,128)S(1)} all-to-all(f32[16,2,16,128]{3,2,1,0:T(8,128)S(1)} %products.6), channel_id=1, replica_groups=mesh['chip'=16,'core'=2,'col'=16] {'chip'}, dimensions={0} | all-to-all | bytes 524288 | tf_op jit(solution)/shard_map/all_to_all | solution.py:270
  126.1 0.3 solve.5
  126.4 20.8 %all_to_all.46.refs_3_ = f32[16,2,16,128]{3,2,1,0:T(8,128)S(1)} all-to-all(f32[16,2,16,128]{3,2,1,0:T(8,128)S(1)} %get-tuple-element.21), channel_id=1, replica_groups=mesh['chip'=16,'core'=2,'col'=16] {'col'}, dimensions={0} | all-to-all | bytes 524288 | tf_op jit(solution)/shard_map/all_to_all | solution.py:263
  147.2 0.8 products.7
  148.0 10.5 %all_to_all.47.received_ref = f32[16,2,16,128]{3,2,1,0:T(8,128)S(1)} all-to-all(f32[16,2,16,128]{3,2,1,0:T(8,128)S(1)} %products.7), channel_id=1, replica_groups=mesh['chip'=16,'core'=2,'col'=16] {'chip'}, dimensions={0} | all-to-all | bytes 524288 | tf_op jit(solution)/shard_map/all_to_all | solution.py:270
  158.5 0.3 last.1
  158.8 1.9 %all-gather.1 = f32[8,16,128]{2,1,0:T(8,128)S(1)} all-gather(f32[4,16,128]{2,1,0:T(8,128)S(1)} %get-tuple-element.26), channel_id=3, replica_groups=mesh['chip'=16,'core'=2,'col'=16] {'core'}, dimensions={0}, use_global_device_ids=true | all-gather | bytes 98304 | tf_op jit(solution)/shard_map/all_gather | solution.py:286
  160.7 0.6 join.1
Async XLA Ops:
  0.0 50.7 %collective-permute-start = (f32[1,1,4,8,128,128]{5,4,3,2,1,0:T(8,128)}, f32[1,1,4,8,128,128]{5,4,3,2,1,0:T(8,128)S(1)}, u32[]{:S(2)}, u32[]{:S(2)}) collective-permute-start(f32[1,1,4,8,128,128]{5,4,3,2,1,0:T(8,128)} %refs_2_.1), channel_id=1, source_target_pairs={{0,16},{16,0},{1,17},{17,1},{2,18},{18,2},{3,19},{19,3},{4,20},{20... | collective-permute-start | bytes 6291464 | tf_op jit(solution)/shard_map/ppermute | solution.py:252

commit v6 on v5

--- a/solution.py
+++ b/solution.py
@@ -12,7 +12,7 @@
 VMEM = pltpu.VMEM
 BASE = 32
 GRANT = 16 << 20
-HEAD_START = 2500
+HEAD_START = 2400
 
 
 def mm(a, b):
@@ -168,20 +168,15 @@
 
 
 def product(operand, block):
-    rows = operand.shape[0]
-    operand_high, operand_low = split(operand)
-    block_high, block_low = split(block)
-    contract = (((1,), (1,)), ((), ()))
-    both = lax.dot_general(
-        jnp.concatenate([operand_high, operand_low], axis=0),
-        block_high,
-        contract,
+    rows, columns = operand.shape[0], block.shape[0]
+    parts = lax.dot_general(
+        jnp.concatenate(split(operand), axis=0),
+        jnp.concatenate(split(block), axis=0),
+        (((1,), (1,)), ((), ())),
         preferred_element_type=jnp.float32,
     )
-    rest = lax.dot_general(
-        operand_high, block_low, contract, preferred_element_type=jnp.float32
-    )
-    return both[:rows] + (both[rows:] + rest)
+    smaller = parts[rows:, :columns] + (parts[:rows, columns:] + parts[rows:, columns:])
+    return parts[:rows, :columns] + smaller
 
 
 def product_kernel(at, tier, both_ref, own_ref, other_ref, *refs):

time: 162 us -> 161 us (level)
  no operation moved by 1% of the time
where the time goes in v6:
time: 161 us; the launch traced here: 160 us
  blocking collectives  130 us (81%)
  Pallas kernels  21.1 us (13%)
  starting transfers between devices  8.73 us (5%)
    all_to_all x4, blocking collectives, per_device(): gathered.append(lax.all_to_all(copies, 'col', 0, 0, tiled=True))  80.3 us
    all_to_all x4, blocking collectives, per_device(): received = lax.all_to_all(partial, 'chip', 0, 0, tiled=True)  45.7 us
    pallas_call x1, Pallas kernels, per_device(): call(functools.partial(spread_kernel, at), copies_shape, (VMEM,), 'spread...  12.2 us
    ppermute x1, starting transfers between devices, per_device(): other_blocks = lax.ppermute(off_blocks, 'core', [(0, 1), (1, 0)])  8.73 us
    pallas_call x1, Pallas kernels, per_device(): call(first_kernel, (shape(at.rows, width), shape(width_rhs, width), shape...  4.79 us
  transfers between devices with their start and end apart: 1, of which 0 were waited for; matrix products, arithmetic and copies ran while one was open for 0% of the time, Pallas kernels for 11%

profile of v6, /device:TPU:1, one launch (start us, length us, event | category | flops | bytes accessed | tf_op | source)
XLA Modules:
  0.0 160.1 jit_solution(9476647961723465178)
XLA Ops:
  0.0 8.7 %collective-permute-start = (f32[1,1,4,8,128,128]{5,4,3,2,1,0:T(8,128)}, f32[1,1,4,8,128,128]{5,4,3,2,1,0:T(8,128)S(1)}, u32[]{:S(2)}, u32[]{:S(2)}) collective-permute-start(f32[1,1,4,8,128,128]{5,4,3,2,1,0:T(8,128)} %refs_2_.1), channel_id=1, source_target_pairs={{0,16},{16,0},{1,17},{17,1},{2,18},{18,2},{3,19},{19,3},{4,20},{20... | collective-permute-start | bytes 6291464 | tf_op jit(solution)/shard_map/ppermute | solution.py:247
  8.7 4.8 %first.1 = (f32[688,128]{1,0:T(8,128)S(1)}, f32[32,128]{1,0:T(8,128)S(1)}, f32[1,1,4,8,128,128]{5,4,3,2,1,0:T(8,128)S(1)}) custom-call(f32[5,1,1,128,128]{4,3,2,1,0:T(8,128)} %refs_0_.1, f32[5,1,1,32,128]{4,3,2,1,0:T(8,128)} %refs_1_.1, f32[1,1,4,8,128,128]{5,4,3,2,1,0:T(8,128)} %refs_2_.1, s32[1,1,4,8]{3,2,1,0:T(4,128)} %refs_3_.1, s32[1,1,4,8]{3,2,1,0:T(4,128)} %refs_4_.1, ...), custom_call_target="tpu_custom_call" | custom-call | flops 67108864 | bytes 1048576 | tf_op jit(solution)/shard_map/first/pallas_call | solution.py:237
  13.5 2.3 %all-gather = f32[1376,128]{1,0:T(8,128)S(1)} all-gather(f32[688,128]{1,0:T(8,128)S(1)} %get-tuple-element.17), channel_id=2, replica_groups=mesh['chip'=16,'core'=2,'col'=16] {'core'}, dimensions={0}, use_global_device_ids=true | all-gather | bytes 1056768 | tf_op jit(solution)/shard_map/all_gather | solution.py:248
  15.9 12.2 %spread.1 = f32[16,2,16,128]{3,2,1,0:T(8,128)S(1)} custom-call(f32[2,688,128]{2,1,0:T(8,128)S(1)} %bitcast.5), custom_call_target="tpu_custom_call" | custom-call | flops 67108864 | bytes 1048576 | tf_op jit(solution)/shard_map/spread/pallas_call | solution.py:249
  28.1 22.1 %all_to_all.40.refs_0_ = f32[16,2,16,128]{3,2,1,0:T(8,128)S(1)} all-to-all(f32[16,2,16,128]{3,2,1,0:T(8,128)S(1)} %spread.1), channel_id=1, replica_groups=mesh['chip'=16,'core'=2,'col'=16] {'col'}, dimensions={0} | all-to-all | bytes 524288 | tf_op jit(solution)/shard_map/all_to_all | solution.py:258
  50.2 0.0 collective-permute-done.other_ref
  50.2 0.5 products.4
  50.7 13.9 %all_to_all.41.received_ref = f32[16,2,16,128]{3,2,1,0:T(8,128)S(1)} all-to-all(f32[16,2,16,128]{3,2,1,0:T(8,128)S(1)} %products.4), channel_id=1, replica_groups=mesh['chip'=16,'core'=2,'col'=16] {'chip'}, dimensions={0} | all-to-all | bytes 524288 | tf_op jit(solution)/shard_map/all_to_all | solution.py:265
  64.6 0.3 solve.3
  65.0 18.6 %all_to_all.42.refs_1_ = f32[16,2,16,128]{3,2,1,0:T(8,128)S(1)} all-to-all(f32[16,2,16,128]{3,2,1,0:T(8,128)S(1)} %get-tuple-element.19), channel_id=1, replica_groups=mesh['chip'=16,'core'=2,'col'=16] {'col'}, dimensions={0} | all-to-all | bytes 524288 | tf_op jit(solution)/shard_map/all_to_all | solution.py:258
  83.6 0.5 products.5
  84.1 10.8 %all_to_all.43.received_ref = f32[16,2,16,128]{3,2,1,0:T(8,128)S(1)} all-to-all(f32[16,2,16,128]{3,2,1,0:T(8,128)S(1)} %products.5), channel_id=1, replica_groups=mesh['chip'=16,'core'=2,'col'=16] {'chip'}, dimensions={0} | all-to-all | bytes 524288 | tf_op jit(solution)/shard_map/all_to_all | solution.py:265
  94.9 0.3 solve.4
  95.2 18.6 %all_to_all.44.refs_2_ = f32[16,2,16,128]{3,2,1,0:T(8,128)S(1)} all-to-all(f32[16,2,16,128]{3,2,1,0:T(8,128)S(1)} %get-tuple-element.20), channel_id=1, replica_groups=mesh['chip'=16,'core'=2,'col'=16] {'col'}, dimensions={0} | all-to-all | bytes 524288 | tf_op jit(solution)/shard_map/all_to_all | solution.py:258
  113.9 0.5 products.6
  114.4 10.5 %all_to_all.45.received_ref = f32[16,2,16,128]{3,2,1,0:T(8,128)S(1)} all-to-all(f32[16,2,16,128]{3,2,1,0:T(8,128)S(1)} %products.6), channel_id=1, replica_groups=mesh['chip'=16,'core'=2,'col'=16] {'chip'}, dimensions={0} | all-to-all | bytes 524288 | tf_op jit(solution)/shard_map/all_to_all | solution.py:265
  124.9 0.3 solve.5
  125.3 20.9 %all_to_all.46.refs_3_ = f32[16,2,16,128]{3,2,1,0:T(8,128)S(1)} all-to-all(f32[16,2,16,128]{3,2,1,0:T(8,128)S(1)} %get-tuple-element.21), channel_id=1, replica_groups=mesh['chip'=16,'core'=2,'col'=16] {'col'}, dimensions={0} | all-to-all | bytes 524288 | tf_op jit(solution)/shard_map/all_to_all | solution.py:258
  146.2 0.5 products.7
  146.8 10.5 %all_to_all.47.received_ref = f32[16,2,16,128]{3,2,1,0:T(8,128)S(1)} all-to-all(f32[16,2,16,128]{3,2,1,0:T(8,128)S(1)} %products.7), channel_id=1, replica_groups=mesh['chip'=16,'core'=2,'col'=16] {'chip'}, dimensions={0} | all-to-all | bytes 524288 | tf_op jit(solution)/shard_map/all_to_all | solution.py:265
  157.3 0.3 last.1
  157.6 1.9 %all-gather.1 = f32[8,16,128]{2,1,0:T(8,128)S(1)} all-gather(f32[4,16,128]{2,1,0:T(8,128)S(1)} %get-tuple-element.26), channel_id=3, replica_groups=mesh['chip'=16,'core'=2,'col'=16] {'core'}, dimensions={0}, use_global_device_ids=true | all-gather | bytes 98304 | tf_op jit(solution)/shard_map/all_gather | solution.py:281
  159.4 0.6 join.1
Async XLA Ops:
  0.0 50.2 %collective-permute-start = (f32[1,1,4,8,128,128]{5,4,3,2,1,0:T(8,128)}, f32[1,1,4,8,128,128]{5,4,3,2,1,0:T(8,128)S(1)}, u32[]{:S(2)}, u32[]{:S(2)}) collective-permute-start(f32[1,1,4,8,128,128]{5,4,3,2,1,0:T(8,128)} %refs_2_.1), channel_id=1, source_target_pairs={{0,16},{16,0},{1,17},{17,1},{2,18},{18,2},{3,19},{19,3},{4,20},{20... | collective-permute-start | bytes 6291464 | tf_op jit(solution)/shard_map/ppermute | solution.py:247

commit v7 on v6

--- a/solution.py
+++ b/solution.py
@@ -48,13 +48,20 @@
         inverses = [v + mm(v, p) for v, p in zip(inverses, powers)]
         span *= 2
     width = BASE
-    while width < size:
+    while 2 * width < size:
         joins = ((rows // (2 * width)) == (cols // (2 * width))) & (
             (rows // width) > (cols // width)
         )
         steps = [mm(jnp.where(joins, m, 0.0), v) for m, v in zip(scaled, inverses)]
         inverses = [v - mm(v, s) for v, s in zip(inverses, steps)]
         width *= 2
+    left = cols[width:] < width
+    steps = [mm(jnp.where(left, m[width:], 0.0), v) for m, v in zip(scaled, inverses)]
+    steps = [jnp.concatenate([jnp.zeros_like(t), t], axis=0) for t in steps]
+    inverses = [
+        jnp.concatenate([v[:width], v[width:] - mm(v[width:], t)], axis=0)
+        for v, t in zip(inverses, steps)
+    ]
     return [v * s for v, s in zip(inverses, scale_cols)]
 
 
@@ -151,15 +158,22 @@
         other_ref[tier] = ref[1 - me]
 
 
-def join_kernel(solved_ref, mine_ref, traded_ref, out_ref):
-    me = lax.axis_index("core")
-    size = mine_ref.shape[1]
-    out_ref[0] = solved_ref[...]
-    for tier in range(mine_ref.shape[0]):
-        out_ref[tier + 1, pl.ds(pl.multiple_of(me * size, size), size)] = mine_ref[tier]
-        out_ref[tier + 1, pl.ds(pl.multiple_of((1 - me) * size, size), size)] = traded_ref[
-            1 - me, tier
-        ]
+def join_kernel(solved_ref, mine_ref, traded_ref, out_ref, sems):
+    me = lax.axis_index("core")
+    tiers, size = mine_ref.shape[:2]
+
+    def half_of(core):
+        return out_ref.at[pl.ds(1, tiers), pl.ds(pl.multiple_of(core * size, size), size)]
+
+    moves = [
+        pltpu.make_async_copy(solved_ref, out_ref.at[0], sems.at[0]),
+        pltpu.make_async_copy(mine_ref, half_of(me), sems.at[1]),
+        pltpu.make_async_copy(traded_ref.at[1 - me], half_of(1 - me), sems.at[2]),
+    ]
+    for move in moves:
+        move.start()
+    for move in moves:
+        move.wait()
 
 
 def split(value):
@@ -279,9 +293,15 @@
         (pltpu.VMEM((2, *half), jnp.float32),),
     )(received, both, *results)
     traded = lax.all_gather(other, "core", axis=0, tiled=False)
-    out = call(join_kernel, shape(level_total, width_rhs, width), (VMEM,) * 3, "join")(
-        first_solved, mine, traded
-    )
+    out = pl.pallas_call(
+        join_kernel,
+        out_shape=shape(level_total, width_rhs, width),
+        in_specs=[pl.BlockSpec(memory_space=VMEM)] * 3,
+        out_specs=pl.BlockSpec(memory_space=pltpu.HBM),
+        scratch_shapes=(pltpu.SemaphoreType.DMA((3,)),),
+        compiler_params=pltpu.CompilerParams(vmem_limit_bytes=GRANT),
+        name="join",
+    )(first_solved, mine, traded)
     return out[:, None, None]
 
 

time: 161 us -> 161 us (level)
  no operation moved by 1% of the time
where the time goes in v7:
time: 161 us; the launch traced here: 160 us
  blocking collectives  130 us (81%)
  Pallas kernels  21.1 us (13%)
  starting transfers between devices  8.73 us (5%)
    all_to_all x4, blocking collectives, per_device(): gathered.append(lax.all_to_all(copies, 'col', 0, 0, tiled=True))  80.3 us
    all_to_all x4, blocking collectives, per_device(): received = lax.all_to_all(partial, 'chip', 0, 0, tiled=True)  45.7 us
    pallas_call x1, Pallas kernels, per_device(): call(functools.partial(spread_kernel, at), copies_shape, (VMEM,), 'spread...  12.2 us
    ppermute x1, starting transfers between devices, per_device(): other_blocks = lax.ppermute(off_blocks, 'core', [(0, 1), (1, 0)])  8.73 us
    pallas_call x1, Pallas kernels, per_device(): call(first_kernel, (shape(at.rows, width), shape(width_rhs, width), shape...  4.76 us
  transfers between devices with their start and end apart: 1, of which 0 were waited for; matrix products, arithmetic and copies ran while one was open for 0% of the time, Pallas kernels for 11%

profile of v7, /device:TPU:1, one launch (start us, length us, event | category | flops | bytes accessed | tf_op | source)
XLA Modules:
  0.0 160.1 jit_solution(11331366126267530670)
XLA Ops:
  0.0 8.7 %collective-permute-start = (f32[1,1,4,8,128,128]{5,4,3,2,1,0:T(8,128)}, f32[1,1,4,8,128,128]{5,4,3,2,1,0:T(8,128)S(1)}, u32[]{:S(2)}, u32[]{:S(2)}) collective-permute-start(f32[1,1,4,8,128,128]{5,4,3,2,1,0:T(8,128)} %refs_2_.1), channel_id=1, source_target_pairs={{0,16},{16,0},{1,17},{17,1},{2,18},{18,2},{3,19},{19,3},{4,20},{20... | collective-permute-start | bytes 6291464 | tf_op jit(solution)/shard_map/ppermute | solution.py:261
  8.7 4.8 %first.1 = (f32[688,128]{1,0:T(8,128)S(1)}, f32[32,128]{1,0:T(8,128)S(1)}, f32[1,1,4,8,128,128]{5,4,3,2,1,0:T(8,128)S(1)}) custom-call(f32[5,1,1,128,128]{4,3,2,1,0:T(8,128)} %refs_0_.1, f32[5,1,1,32,128]{4,3,2,1,0:T(8,128)} %refs_1_.1, f32[1,1,4,8,128,128]{5,4,3,2,1,0:T(8,128)} %refs_2_.1, s32[1,1,4,8]{3,2,1,0:T(4,128)} %refs_3_.1, s32[1,1,4,8]{3,2,1,0:T(4,128)} %refs_4_.1, ...), custom_call_target="tpu_custom_call" | custom-call | flops 67108864 | bytes 1048576 | tf_op jit(solution)/shard_map/first/pallas_call | solution.py:251
  13.5 2.3 %all-gather = f32[1376,128]{1,0:T(8,128)S(1)} all-gather(f32[688,128]{1,0:T(8,128)S(1)} %get-tuple-element.17), channel_id=2, replica_groups=mesh['chip'=16,'core'=2,'col'=16] {'core'}, dimensions={0}, use_global_device_ids=true | all-gather | bytes 1056768 | tf_op jit(solution)/shard_map/all_gather | solution.py:262
  15.8 12.2 %spread.1 = f32[16,2,16,128]{3,2,1,0:T(8,128)S(1)} custom-call(f32[2,688,128]{2,1,0:T(8,128)S(1)} %bitcast.5), custom_call_target="tpu_custom_call" | custom-call | flops 67108864 | bytes 1048576 | tf_op jit(solution)/shard_map/spread/pallas_call | solution.py:263
  28.1 22.1 %all_to_all.40.refs_0_ = f32[16,2,16,128]{3,2,1,0:T(8,128)S(1)} all-to-all(f32[16,2,16,128]{3,2,1,0:T(8,128)S(1)} %spread.1), channel_id=1, replica_groups=mesh['chip'=16,'core'=2,'col'=16] {'col'}, dimensions={0} | all-to-all | bytes 524288 | tf_op jit(solution)/shard_map/all_to_all | solution.py:272
  50.2 0.0 collective-permute-done.other_ref
  50.2 0.5 products.4
  50.7 13.9 %all_to_all.41.received_ref = f32[16,2,16,128]{3,2,1,0:T(8,128)S(1)} all-to-all(f32[16,2,16,128]{3,2,1,0:T(8,128)S(1)} %products.4), channel_id=1, replica_groups=mesh['chip'=16,'core'=2,'col'=16] {'chip'}, dimensions={0} | all-to-all | bytes 524288 | tf_op jit(solution)/shard_map/all_to_all | solution.py:279
  64.6 0.3 solve.3
  64.9 18.6 %all_to_all.42.refs_1_ = f32[16,2,16,128]{3,2,1,0:T(8,128)S(1)} all-to-all(f32[16,2,16,128]{3,2,1,0:T(8,128)S(1)} %get-tuple-element.19), channel_id=1, replica_groups=mesh['chip'=16,'core'=2,'col'=16] {'col'}, dimensions={0} | all-to-all | bytes 524288 | tf_op jit(solution)/shard_map/all_to_all | solution.py:272
  83.5 0.5 products.5
  84.1 10.8 %all_to_all.43.received_ref = f32[16,2,16,128]{3,2,1,0:T(8,128)S(1)} all-to-all(f32[16,2,16,128]{3,2,1,0:T(8,128)S(1)} %products.5), channel_id=1, replica_groups=mesh['chip'=16,'core'=2,'col'=16] {'chip'}, dimensions={0} | all-to-all | bytes 524288 | tf_op jit(solution)/shard_map/all_to_all | solution.py:279
  94.9 0.3 solve.4
  95.2 18.6 %all_to_all.44.refs_2_ = f32[16,2,16,128]{3,2,1,0:T(8,128)S(1)} all-to-all(f32[16,2,16,128]{3,2,1,0:T(8,128)S(1)} %get-tuple-element.20), channel_id=1, replica_groups=mesh['chip'=16,'core'=2,'col'=16] {'col'}, dimensions={0} | all-to-all | bytes 524288 | tf_op jit(solution)/shard_map/all_to_all | solution.py:272
  113.8 0.5 products.6
  114.4 10.5 %all_to_all.45.received_ref = f32[16,2,16,128]{3,2,1,0:T(8,128)S(1)} all-to-all(f32[16,2,16,128]{3,2,1,0:T(8,128)S(1)} %products.6), channel_id=1, replica_groups=mesh['chip'=16,'core'=2,'col'=16] {'chip'}, dimensions={0} | all-to-all | bytes 524288 | tf_op jit(solution)/shard_map/all_to_all | solution.py:279
  124.9 0.3 solve.5
  125.2 20.9 %all_to_all.46.refs_3_ = f32[16,2,16,128]{3,2,1,0:T(8,128)S(1)} all-to-all(f32[16,2,16,128]{3,2,1,0:T(8,128)S(1)} %get-tuple-element.21), channel_id=1, replica_groups=mesh['chip'=16,'core'=2,'col'=16] {'col'}, dimensions={0} | all-to-all | bytes 524288 | tf_op jit(solution)/shard_map/all_to_all | solution.py:272
  146.2 0.5 products.7
  146.7 10.5 %all_to_all.47.received_ref = f32[16,2,16,128]{3,2,1,0:T(8,128)S(1)} all-to-all(f32[16,2,16,128]{3,2,1,0:T(8,128)S(1)} %products.7), channel_id=1, replica_groups=mesh['chip'=16,'core'=2,'col'=16] {'chip'}, dimensions={0} | all-to-all | bytes 524288 | tf_op jit(solution)/shard_map/all_to_all | solution.py:279
  157.2 0.3 last.1
  157.5 1.9 %all-gather.1 = f32[8,16,128]{2,1,0:T(8,128)S(1)} all-gather(f32[4,16,128]{2,1,0:T(8,128)S(1)} %get-tuple-element.26), channel_id=3, replica_groups=mesh['chip'=16,'core'=2,'col'=16] {'core'}, dimensions={0}, use_global_device_ids=true | all-gather | bytes 98304 | tf_op jit(solution)/shard_map/all_gather | solution.py:295
  159.4 0.7 join.1
Async XLA Ops:
  0.0 50.2 %collective-permute-start = (f32[1,1,4,8,128,128]{5,4,3,2,1,0:T(8,128)}, f32[1,1,4,8,128,128]{5,4,3,2,1,0:T(8,128)S(1)}, u32[]{:S(2)}, u32[]{:S(2)}) collective-permute-start(f32[1,1,4,8,128,128]{5,4,3,2,1,0:T(8,128)} %refs_2_.1), channel_id=1, source_target_pairs={{0,16},{16,0},{1,17},{17,1},{2,18},{18,2},{3,19},{19,3},{4,20},{20... | collective-permute-start | bytes 6291464 | tf_op jit(solution)/shard_map/ppermute | solution.py:261

commit v8 on v7

--- a/solution.py
+++ b/solution.py
@@ -12,7 +12,7 @@
 VMEM = pltpu.VMEM
 BASE = 32
 GRANT = 16 << 20
-HEAD_START = 2400
+HEAD_START = 2350
 
 
 def mm(a, b):

time: 161 us -> 161 us (level)
  transfers between devices with their start and end apart: 1 -> 1, of which waited for: 0 -> 0; matrix products, arithmetic and copies ran while one was open for 0% -> 0% of each run, Pallas kernels for 11% -> 10%
where the time goes in v8:
time: 161 us; the launch traced here: 160 us
  blocking collectives  131 us (81%)
  Pallas kernels  20.8 us (13%)
  starting transfers between devices  8.73 us (5%)
    all_to_all x4, blocking collectives, per_device(): gathered.append(lax.all_to_all(copies, 'col', 0, 0, tiled=True))  80.8 us
    all_to_all x4, blocking collectives, per_device(): received = lax.all_to_all(partial, 'chip', 0, 0, tiled=True)  45.6 us
    pallas_call x1, Pallas kernels, per_device(): call(functools.partial(spread_kernel, at), copies_shape, (VMEM,), 'spread...  12 us
    ppermute x1, starting transfers between devices, per_device(): other_blocks = lax.ppermute(off_blocks, 'core', [(0, 1), (1, 0)])  8.73 us
    pallas_call x1, Pallas kernels, per_device(): call(first_kernel, (shape(at.rows, width), shape(width_rhs, width), shape...  4.76 us
  transfers between devices with their start and end apart: 1, of which 0 were waited for; matrix products, arithmetic and copies ran while one was open for 0% of the time, Pallas kernels for 10%

profile of v8, /device:TPU:1, one launch (start us, length us, event | category | flops | bytes accessed | tf_op | source)
XLA Modules:
  0.0 160.2 jit_solution(14448016224842397476)
XLA Ops:
  0.0 8.7 %collective-permute-start = (f32[1,1,4,8,128,128]{5,4,3,2,1,0:T(8,128)}, f32[1,1,4,8,128,128]{5,4,3,2,1,0:T(8,128)S(1)}, u32[]{:S(2)}, u32[]{:S(2)}) collective-permute-start(f32[1,1,4,8,128,128]{5,4,3,2,1,0:T(8,128)} %refs_2_.1), channel_id=1, source_target_pairs={{0,16},{16,0},{1,17},{17,1},{2,18},{18,2},{3,19},{19,3},{4,20},{20... | collective-permute-start | bytes 6291464 | tf_op jit(solution)/shard_map/ppermute | solution.py:261
  8.7 4.8 %first.1 = (f32[688,128]{1,0:T(8,128)S(1)}, f32[32,128]{1,0:T(8,128)S(1)}, f32[1,1,4,8,128,128]{5,4,3,2,1,0:T(8,128)S(1)}) custom-call(f32[5,1,1,128,128]{4,3,2,1,0:T(8,128)} %refs_0_.1, f32[5,1,1,32,128]{4,3,2,1,0:T(8,128)} %refs_1_.1, f32[1,1,4,8,128,128]{5,4,3,2,1,0:T(8,128)} %refs_2_.1, s32[1,1,4,8]{3,2,1,0:T(4,128)} %refs_3_.1, s32[1,1,4,8]{3,2,1,0:T(4,128)} %refs_4_.1, ...), custom_call_target="tpu_custom_call" | custom-call | flops 67108864 | bytes 1048576 | tf_op jit(solution)/shard_map/first/pallas_call | solution.py:251
  13.5 2.3 %all-gather = f32[1376,128]{1,0:T(8,128)S(1)} all-gather(f32[688,128]{1,0:T(8,128)S(1)} %get-tuple-element.17), channel_id=2, replica_groups=mesh['chip'=16,'core'=2,'col'=16] {'core'}, dimensions={0}, use_global_device_ids=true | all-gather | bytes 1056768 | tf_op jit(solution)/shard_map/all_gather | solution.py:262
  15.8 12.0 %spread.1 = f32[16,2,16,128]{3,2,1,0:T(8,128)S(1)} custom-call(f32[2,688,128]{2,1,0:T(8,128)S(1)} %bitcast.5), custom_call_target="tpu_custom_call" | custom-call | flops 67108864 | bytes 1048576 | tf_op jit(solution)/shard_map/spread/pallas_call | solution.py:263
  27.8 22.1 %all_to_all.40.refs_0_ = f32[16,2,16,128]{3,2,1,0:T(8,128)S(1)} all-to-all(f32[16,2,16,128]{3,2,1,0:T(8,128)S(1)} %spread.1), channel_id=1, replica_groups=mesh['chip'=16,'core'=2,'col'=16] {'col'}, dimensions={0} | all-to-all | bytes 524288 | tf_op jit(solution)/shard_map/all_to_all | solution.py:272
  49.9 0.0 collective-permute-done.other_ref
  49.9 0.5 products.4
  50.4 13.9 %all_to_all.41.received_ref = f32[16,2,16,128]{3,2,1,0:T(8,128)S(1)} all-to-all(f32[16,2,16,128]{3,2,1,0:T(8,128)S(1)} %products.4), channel_id=1, replica_groups=mesh['chip'=16,'core'=2,'col'=16] {'chip'}, dimensions={0} | all-to-all | bytes 524288 | tf_op jit(solution)/shard_map/all_to_all | solution.py:279
  64.3 0.3 solve.3
  64.7 18.7 %all_to_all.42.refs_1_ = f32[16,2,16,128]{3,2,1,0:T(8,128)S(1)} all-to-all(f32[16,2,16,128]{3,2,1,0:T(8,128)S(1)} %get-tuple-element.19), channel_id=1, replica_groups=mesh['chip'=16,'core'=2,'col'=16] {'col'}, dimensions={0} | all-to-all | bytes 524288 | tf_op jit(solution)/shard_map/all_to_all | solution.py:272
  83.4 0.5 products.5
  83.9 10.7 %all_to_all.43.received_ref = f32[16,2,16,128]{3,2,1,0:T(8,128)S(1)} all-to-all(f32[16,2,16,128]{3,2,1,0:T(8,128)S(1)} %products.5), channel_id=1, replica_groups=mesh['chip'=16,'core'=2,'col'=16] {'chip'}, dimensions={0} | all-to-all | bytes 524288 | tf_op jit(solution)/shard_map/all_to_all | solution.py:279
  94.6 0.3 solve.4
  94.9 19.3 %all_to_all.44.refs_2_ = f32[16,2,16,128]{3,2,1,0:T(8,128)S(1)} all-to-all(f32[16,2,16,128]{3,2,1,0:T(8,128)S(1)} %get-tuple-element.20), channel_id=1, replica_groups=mesh['chip'=16,'core'=2,'col'=16] {'col'}, dimensions={0} | all-to-all | bytes 524288 | tf_op jit(solution)/shard_map/all_to_all | solution.py:272
  114.2 0.5 products.6
  114.7 10.5 %all_to_all.45.received_ref = f32[16,2,16,128]{3,2,1,0:T(8,128)S(1)} all-to-all(f32[16,2,16,128]{3,2,1,0:T(8,128)S(1)} %products.6), channel_id=1, replica_groups=mesh['chip'=16,'core'=2,'col'=16] {'chip'}, dimensions={0} | all-to-all | bytes 524288 | tf_op jit(solution)/shard_map/all_to_all | solution.py:279
  125.3 0.3 solve.5
  125.6 20.7 %all_to_all.46.refs_3_ = f32[16,2,16,128]{3,2,1,0:T(8,128)S(1)} all-to-all(f32[16,2,16,128]{3,2,1,0:T(8,128)S(1)} %get-tuple-element.21), channel_id=1, replica_groups=mesh['chip'=16,'core'=2,'col'=16] {'col'}, dimensions={0} | all-to-all | bytes 524288 | tf_op jit(solution)/shard_map/all_to_all | solution.py:272
  146.3 0.5 products.7
  146.9 10.5 %all_to_all.47.received_ref = f32[16,2,16,128]{3,2,1,0:T(8,128)S(1)} all-to-all(f32[16,2,16,128]{3,2,1,0:T(8,128)S(1)} %products.7), channel_id=1, replica_groups=mesh['chip'=16,'core'=2,'col'=16] {'chip'}, dimensions={0} | all-to-all | bytes 524288 | tf_op jit(solution)/shard_map/all_to_all | solution.py:279
  157.4 0.3 last.1
  157.7 1.9 %all-gather.1 = f32[8,16,128]{2,1,0:T(8,128)S(1)} all-gather(f32[4,16,128]{2,1,0:T(8,128)S(1)} %get-tuple-element.26), channel_id=3, replica_groups=mesh['chip'=16,'core'=2,'col'=16] {'core'}, dimensions={0}, use_global_device_ids=true | all-gather | bytes 98304 | tf_op jit(solution)/shard_map/all_gather | solution.py:295
  159.5 0.7 join.1
Async XLA Ops:
  0.0 49.9 %collective-permute-start = (f32[1,1,4,8,128,128]{5,4,3,2,1,0:T(8,128)}, f32[1,1,4,8,128,128]{5,4,3,2,1,0:T(8,128)S(1)}, u32[]{:S(2)}, u32[]{:S(2)}) collective-permute-start(f32[1,1,4,8,128,128]{5,4,3,2,1,0:T(8,128)} %refs_2_.1), channel_id=1, source_target_pairs={{0,16},{16,0},{1,17},{17,1},{2,18},{18,2},{3,19},{19,3},{4,20},{20... | collective-permute-start | bytes 6291464 | tf_op jit(solution)/shard_map/ppermute | solution.py:261
